TPU v7x, 8 devices: a whole 2x2x1 slice. The times are simulated.
8 devices in a mesh: dp: 1 (over z), embed: 2 (over y), heads: 4 (over x, core).
Axes of the slice: x: 2, y: 2, z: 1, core: 2. Of those that a mesh axis runs over, the one named last changes fastest.
Arguments:
- x_in: bfloat16 [256, 3072], P('dp', 'embed')
- positions: int32 [256], P('dp')
- gain_one: float32 [3072], P('embed')
- gain_two: float32 [3072], P('embed')
- w_qkv: bfloat16 [3072, 32, 288], P('embed', 'heads')
- w_out: bfloat16 [3072, 3072], P('heads', 'embed')
- w_gu: bfloat16 [3072, 2, 8192], P('embed', None, 'heads')
- w_down: bfloat16 [8192, 3072], P('heads', 'embed')
- grad_out: bfloat16 [256, 3072], P('dp', 'embed')
Outputs:
- output 1: bfloat16 [256, 3072], P('dp', 'embed')
- output 2: bfloat16 [256, 3072], P('dp', 'embed')
- output 3: float32 [3072], P(('dp', 'embed'))
- output 4: float32 [3072], P(('dp', 'embed'))
- output 5: float32 [3072, 32, 288], P(('dp', 'embed'), 'heads')
- output 6: float32 [3072, 3072], P(('dp', 'heads'), 'embed')
- output 7: float32 [3072, 2, 8192], P(('dp', 'embed'), None, 'heads')
- output 8: float32 [8192, 3072], P(('dp', 'heads'), 'embed')
All inputs are finite; a program needn't handle non-finite values.
Results may differ from a plain program's by a relative error of at most 0.02.
Values are sent between devices in bfloat16 or wider.
A program may use at most 1 GiB of HBM per device.

v0:
```python
import jax
import jax.numpy as jnp
from jax import lax
from jax.sharding import PartitionSpec as P

EPSILON = 1e-5
ROPE_BASE = 10000.0


def rope_tables(positions, head_dim):
    inv_freq = ROPE_BASE ** (-jnp.arange(0, head_dim, 2, dtype=jnp.float32) / head_dim)
    angles = positions.astype(jnp.float32)[:, None] * inv_freq[None, :]
    angles = jnp.concatenate([angles, angles], axis=-1)
    return jnp.cos(angles), jnp.sin(angles)


def apply_rope(operand, cos_t, sin_t):
    half_dim = operand.shape[-1] // 2
    operand = operand.astype(jnp.float32)
    rotated = jnp.concatenate([-operand[..., half_dim:], operand[..., :half_dim]], axis=-1)
    return (operand * cos_t + rotated * sin_t).astype(jnp.bfloat16)


def attention_core(packed, cos_t, sin_t, head_dim):
    num_seqs, seq_len, groups, qkv_width = packed.shape
    q_per_kv = qkv_width // head_dim - 2
    q_cut = q_per_kv * head_dim
    queries = apply_rope(packed[..., :q_cut].reshape(num_seqs, seq_len, groups, q_per_kv, head_dim), cos_t[:, None, None, :], sin_t[:, None, None, :])
    key_rot = apply_rope(packed[..., q_cut:q_cut + head_dim], cos_t[:, None, :], sin_t[:, None, :])
    values = packed[..., q_cut + head_dim:]
    scores = jnp.einsum('bqkgh,bskh->bkgqs', queries, key_rot, preferred_element_type=jnp.float32)
    causal = jnp.arange(seq_len)[:, None] >= jnp.arange(seq_len)[None, :]
    scores = jnp.where(causal, scores * head_dim ** -0.5, -1e30)
    attn_probs = jax.nn.softmax(scores, axis=-1).astype(jnp.bfloat16)
    attn_mix = jnp.einsum('bkgqs,bskh->bqkgh', attn_probs, values, preferred_element_type=jnp.float32)
    return attn_mix.astype(jnp.bfloat16).reshape(num_seqs, seq_len, groups * q_cut)


def swiglu(gate_up):
    gate_up = gate_up.astype(jnp.float32)
    return (jax.nn.silu(gate_up[:, 0]) * gate_up[:, 1]).astype(jnp.bfloat16)


def rms_forward(hidden, gain, sum_width, full_width):
    hidden32 = hidden.astype(jnp.float32)
    sq_sum = sum_width(jnp.sum(hidden32 * hidden32, axis=-1, keepdims=True))
    inv_rms = lax.rsqrt(sq_sum / full_width + EPSILON)
    unit_rows = hidden32 * inv_rms
    return (unit_rows * gain).astype(jnp.bfloat16), unit_rows, inv_rms


def rms_backward(grad_normed, unit_rows, inv_rms, gain, sum_width, full_width):
    grad_in = grad_normed.astype(jnp.float32)
    grad_gain = jnp.sum(grad_in * unit_rows, axis=0)
    scaled = grad_in * gain
    dot_sum = sum_width(jnp.sum(scaled * unit_rows, axis=-1, keepdims=True))
    return inv_rms * (scaled - unit_rows * (dot_sum / full_width)), grad_gain


def layer_step(x_in, positions, gain_one, gain_two, w_qkv, w_out, w_gu, w_down, grad_out, sum_embed, sum_heads, full_width):
    seq_len = positions.shape[0]
    tokens = x_in.shape[0]
    num_seqs = tokens // seq_len
    groups, qkv_width = w_qkv.shape[1], w_qkv.shape[2]
    q_cut = w_out.shape[0] // groups
    head_dim = (qkv_width - q_cut) // 2
    cos_t, sin_t = rope_tables(positions, head_dim)
    normed_one, unit_one, inv_one = rms_forward(x_in, gain_one, sum_embed, full_width)
    qkv_all = sum_embed(jnp.einsum('td,dgc->tgc', normed_one, w_qkv, preferred_element_type=jnp.float32).astype(jnp.bfloat16))
    attn_mix, attn_vjp = jax.vjp(lambda packed: attention_core(packed, cos_t, sin_t, head_dim), qkv_all.reshape(num_seqs, seq_len, groups, qkv_width))
    attn_mix = attn_mix.reshape(tokens, groups * q_cut)
    attn_out = sum_heads(jnp.dot(attn_mix, w_out, preferred_element_type=jnp.float32).astype(jnp.bfloat16))
    hidden = (x_in.astype(jnp.float32) + attn_out.astype(jnp.float32)).astype(jnp.bfloat16)
    normed_two, unit_two, inv_two = rms_forward(hidden, gain_two, sum_embed, full_width)
    gate_up = sum_embed(jnp.einsum('td,dkf->tkf', normed_two, w_gu, preferred_element_type=jnp.float32).astype(jnp.bfloat16))
    act_out, act_vjp = jax.vjp(swiglu, gate_up)
    mlp_out = sum_heads(jnp.dot(act_out, w_down, preferred_element_type=jnp.float32).astype(jnp.bfloat16))
    y_out = (hidden.astype(jnp.float32) + mlp_out.astype(jnp.float32)).astype(jnp.bfloat16)

    grad_w_down = jnp.einsum('tf,td->fd', act_out, grad_out, preferred_element_type=jnp.float32)
    grad_act = sum_embed(jnp.einsum('td,fd->tf', grad_out, w_down, preferred_element_type=jnp.float32).astype(jnp.bfloat16))
    (grad_gate_up,) = act_vjp(grad_act)
    grad_w_gu = jnp.einsum('td,tkf->dkf', normed_two, grad_gate_up, preferred_element_type=jnp.float32)
    grad_normed_two = sum_heads(jnp.einsum('tkf,dkf->td', grad_gate_up, w_gu, preferred_element_type=jnp.float32).astype(jnp.bfloat16))
    grad_hidden_norm, grad_gain_two = rms_backward(grad_normed_two, unit_two, inv_two, gain_two, sum_embed, full_width)
    grad_hidden = (grad_out.astype(jnp.float32) + grad_hidden_norm).astype(jnp.bfloat16)
    grad_w_out = jnp.einsum('ta,td->ad', attn_mix, grad_hidden, preferred_element_type=jnp.float32)
    grad_mix = sum_embed(jnp.einsum('td,ad->ta', grad_hidden, w_out, preferred_element_type=jnp.float32).astype(jnp.bfloat16))
    (grad_qkv,) = attn_vjp(grad_mix.reshape(num_seqs, seq_len, groups * q_cut))
    grad_qkv = grad_qkv.reshape(tokens, groups, qkv_width)
    grad_w_qkv = jnp.einsum('td,tgc->dgc', normed_one, grad_qkv, preferred_element_type=jnp.float32)
    grad_normed_one = sum_heads(jnp.einsum('tgc,dgc->td', grad_qkv, w_qkv, preferred_element_type=jnp.float32).astype(jnp.bfloat16))
    grad_x_norm, grad_gain_one = rms_backward(grad_normed_one, unit_one, inv_one, gain_one, sum_embed, full_width)
    grad_x = (grad_hidden.astype(jnp.float32) + grad_x_norm).astype(jnp.bfloat16)
    return (y_out, grad_x, grad_gain_one, grad_gain_two, grad_w_qkv, grad_w_out, grad_w_gu, grad_w_down)


def sum_over_embed(partial_sum):
    return lax.psum(partial_sum, 'embed')


def sum_over_heads(partial_sum):
    return lax.psum(partial_sum, 'heads')


def solution(mesh):
    embed_size = mesh.shape['embed']

    def per_device(x_in, positions, gain_one, gain_two, w_qkv, w_out, w_gu, w_down, grad_out):
        full_width = x_in.shape[1] * embed_size
        return layer_step(x_in, positions, gain_one, gain_two, w_qkv, w_out, w_gu, w_down, grad_out, sum_over_embed, sum_over_heads, full_width)

    act_spec = P('dp', 'embed')
    in_specs = (act_spec, P('dp'), P('embed'), P('embed'), P('embed', 'heads', None), P('heads', 'embed'), P('embed', None, 'heads'), P('heads', 'embed'), act_spec)
    out_specs = (act_spec, act_spec, P(('dp', 'embed')), P(('dp', 'embed')), P(('dp', 'embed'), 'heads', None), P(('dp', 'heads'), 'embed'), P(('dp', 'embed'), None, 'heads'), P(('dp', 'heads'), 'embed'))
    return jax.shard_map(per_device, mesh=mesh, in_specs=in_specs, out_specs=out_specs, check_vma=False)
```

profile of v0, /device:TPU:0, one launch (start us, length us, event | category | flops | bytes accessed | tf_op | source)
XLA Modules:
  0.0 405.1 jit_solution(15877207719372831200)
XLA Ops:
  7.2 1.5 fusion.48
  8.7 6.3 %psum.84 = f32[256,1]{0,1:T(1,128)S(1)} all-reduce(f32[256,1]{0,1:T(1,128)S(1)} %bitcast.209), channel_id=1, replica_groups=mesh['dp'=1,'embed'=2,'heads'=4] {'embed'}, use_global_device_ids=true, to_apply=%region_1.0 | all-reduce | flops 256 | bytes 2048 | tf_op jit(solution)/shard_map/psum | solution.py:99
  15.0 6.4 %fusion.55 = bf16[1,256,8,288]{1,3,2,0:T(8,128)(2,1)} fusion(bf16[1536,8,288]{0,2,1:T(8,128)(2,1)} %param.13, bf16[256,1536]{1,0:T(8,128)(2,1)} %param.9, f32[1536]{0:T(1024)} %param.11, f32[256]{0:T(256)S(1)} %bitcast.200), kind=kOutput, calls=%fused_computation.76 | convolution fusion | flops 1814102016 | bytes 9051136 | tf_op jit(solution)/shard_map/td,dgc->tgc/dot_general | solution.py:69
  21.6 0.1 broadcast_multiply_fusion
  21.7 0.4 fusion.88
  22.1 38.2 %all-reduce.18.cloned.1.call-done = bf16[1,256,8,288]{1,3,2,0:T(8,128)(2,1)} async-done(((bf16[1,256,8,288]{1,3,2,0:T(8,128)(2,1)}), bf16[1,256,8,288]{1,3,2,0:T(8,128)(2,1)}) %all-reduce.18.cloned.1.call-update) | async-done | bytes 1179664 | tf_op jit(solution)/shard_map/psum | solution.py:99
  60.3 1.3 convert_bitcast_fusion
  61.6 0.1 fusion.86
  61.6 0.1 slice_negate_fusion.3
  61.7 1.1 copy-done.10
  62.8 0.1 fusion.68
  63.0 0.1 fusion.85
  63.2 0.5 fusion.38
  63.7 0.4 fusion.89
  64.2 1.6 convolution_convert_fusion.9
  65.9 1.7 convolution_convert_fusion
  67.6 5.6 %convolution_convert_fusion.1 = bf16[256,2048]{1,0:T(8,128)(2,1)} fusion(bf16[256,1536]{1,0:T(8,128)(2,1)S(1)} %copy-done.5, bf16[2048,1536]{1,0:T(8,128)(2,1)} %param.16), kind=kOutput, calls=%fused_computation.15 | convolution fusion | flops 1611137024 | bytes 8126464 | tf_op jit(solution)/shard_map/td,fd->tf/dot_general | solution.py:81
  73.2 23.8 %all-reduce.20.cloned.1.call-done = bf16[256,1536]{1,0:T(8,128)(2,1)} async-done(((bf16[256,1536]{1,0:T(8,128)(2,1)}), bf16[256,1536]{1,0:T(8,128)(2,1)}) %all-reduce.20.cloned.1.call-update) | async-done | bytes 786448 | tf_op jit(solution)/shard_map/psum | solution.py:103
  97.1 2.3 fusion.53
  99.4 5.8 %psum.87 = f32[256,1]{0,1:T(1,128)} all-reduce(f32[256,1]{0,1:T(1,128)} %bitcast.205), channel_id=1, replica_groups=mesh['dp'=1,'embed'=2,'heads'=4] {'embed'}, use_global_device_ids=true, to_apply=%region_7.8 | all-reduce | flops 256 | bytes 2048 | tf_op jit(solution)/shard_map/psum | solution.py:99
  105.1 0.7 add_rsqrt_fusion
  105.8 0.6 copy-done.29
  106.4 14.3 %fusion.4 = bf16[256,2,2048]{2,0,1:T(8,128)(2,1)} fusion(bf16[1536,2,2048]{2,1,0:T(2,128)(2,1)} %param.15, bf16[256,1536]{1,0:T(8,128)(2,1)S(1)} %get-tuple-element.33, f32[1536]{0:T(1024)S(1)} %copy-done.25, f32[256]{0:T(256)S(1)} %bitcast.196), kind=kOutput, calls=%fused_computation.6 | convolution fusion | flops 3223846912 | bytes 15473664 | tf_op jit(solution)/shard_map/td,dkf->tkf/dot_general | solution.py:75
  120.8 1.3 multiply_divide_fusion
  122.1 78.8 %all-reduce.28.cloned.1.call-done = (bf16[256,2,2048]{2,0,1:T(8,128)(2,1)}, bf16[256,2048]{1,0:T(8,128)(2,1)}) async-done(((bf16[256,2,2048]{2,0,1:T(8,128)(2,1)}, bf16[256,2048]{1,0:T(8,128)(2,1)}), (bf16[256,2,2048]{2,0,1:T(8,128)(2,1)}, bf16[256,2048]{1,0:T(8,128)(2,1)})) %all-reduce.28.cloned.1.call-update) | async-done | bytes 3145744 | tf_op jit(solution)/shard_map/psum | solution.py:99
  200.9 2.2 convert_element_type.199
  203.1 2.2 fusion.22
  205.3 10.5 %fusion.81 = f32[1536,2,2048]{2,0,1:T(8,128)} fusion(bf16[256,1536]{1,0:T(8,128)(2,1)S(1)} %get-tuple-element.33, f32[1536]{0:T(1024)S(1)} %copy-done.25, f32[256]{0:T(256)S(1)} %bitcast.199, f32[256,1,2048]{2,0,1:T(8,128)S(1)} %get-tuple-element.35, f32[256,1,2048]{2,0,1:T(8,128)S(1)} %get-tuple-element.34), kind=kOutput, calls=%fused_computation.112 | convolution fusion | flops 3224895488 | bytes 30153728 | tf_op jit(solution)/shard_map/td,tkf->dkf/dot_general | solution.py:83
  215.8 13.8 %fusion.11 = bf16[256,1536]{1,0:T(8,128)(2,1)} fusion(bf16[1536,2,2048]{2,1,0:T(2,128)(2,1)} %param.15, f32[256,1,2048]{2,0,1:T(8,128)S(1)} %get-tuple-element.35, f32[256,1,2048]{2,0,1:T(8,128)S(1)} %get-tuple-element.34), kind=kOutput, calls=%fused_computation.17 | convolution fusion | flops 3223715840 | bytes 17563648 | tf_op jit(solution)/shard_map/tkf,dkf->td/dot_general | solution.py:84
  229.6 41.8 %copy.30 = f32[1536,2,2048]{2,1,0:T(2,128)} copy(f32[1536,2,2048]{2,0,1:T(8,128)} %fusion.81) | data formatting | bytes 50331648
  271.4 0.3 all-reduce.24.cloned.1.call-start
  271.7 8.1 %fusion.104 = f32[2048,1536]{1,0:T(8,128)} fusion(bf16[256,2048]{1,0:T(8,128)(2,1)} %get-tuple-element.36, bf16[256,1536]{1,0:T(8,128)(2,1)} %param.17), kind=kOutput, calls=%fused_computation.148 | convolution fusion | flops 1610612736 | bytes 14417920 | tf_op jit(solution)/shard_map/tf,td->fd/dot_general | solution.py:80
  279.8 21.2 %all-reduce.22.cloned.1.call-done = bf16[256,1536]{1,0:T(8,128)(2,1)} async-done(((bf16[256,1536]{1,0:T(8,128)(2,1)}), bf16[256,1536]{1,0:T(8,128)(2,1)}) %all-reduce.22.cloned.1.call-update) | async-done | bytes 786448 | tf_op jit(solution)/shard_map/psum | solution.py:103
  301.0 2.4 fusion.52
  303.4 5.6 %psum.92 = f32[256,1]{0,1:T(1,128)} all-reduce(f32[256,1]{0,1:T(1,128)} %bitcast.207), channel_id=1, replica_groups=mesh['dp'=1,'embed'=2,'heads'=4] {'embed'}, use_global_device_ids=true, to_apply=%region_13.14 | all-reduce | flops 256 | bytes 2048 | tf_op jit(solution)/shard_map/psum | solution.py:99
  309.0 0.7 broadcast_multiply_fusion.2
  309.7 1.9 fusion.44
  311.6 0.9 copy-done.4
  312.5 1.6 convolution_convert_fusion.8
  314.1 1.9 copy.27
  316.1 5.8 %convolution_convert_fusion.2 = bf16[256,1536]{1,0:T(8,128)(2,1)} fusion(bf16[256,2048]{1,0:T(8,128)(2,1)} %get-tuple-element.36, bf16[2048,1536]{1,0:T(8,128)(2,1)} %param.16), kind=kOutput, calls=%fused_computation.16 | convolution fusion | flops 1611005952 | bytes 8126464 | tf_op jit(solution)/shard_map/dot_general | solution.py:77
  321.8 14.3 %all-reduce.24.cloned.1.call-done = bf16[8,96,256]{2,1,0:T(8,128)(2,1)} async-done(((bf16[8,96,256]{2,1,0:T(8,128)(2,1)}), bf16[8,96,256]{2,1,0:T(8,128)(2,1)}) %all-reduce.24.cloned.1.call-update) | async-done | bytes 393232 | tf_op jit(solution)/shard_map/psum | solution.py:99
  336.2 2.8 fusion.31
  339.1 1.0 fusion.58
  340.1 1.0 fusion.60
  341.2 0.1 multiply_bitcast_fusion.1
  341.2 0.1 fusion.101
  341.3 0.1 multiply_bitcast_fusion
  341.4 0.1 fusion.102
  341.5 0.7 copy-done.7
  342.1 0.2 fusion.76
  342.3 0.2 fusion.84
  342.5 0.7 fusion.56
  343.3 0.8 copy-done.23
  344.0 0.7 slice-done
  344.8 0.9 slice-done.1
  345.7 2.9 fusion.10
  348.6 4.2 %fusion.103 = f32[768,1536]{1,0:T(8,128)} fusion(bf16[256,768]{0,1:T(8,128)(2,1)S(1)} %bitcast.194, bf16[256,1536]{1,0:T(8,128)(2,1)} %copy-done.4), kind=kOutput, calls=%fused_computation.147 | convolution fusion | flops 603979776 | bytes 5898240 | tf_op jit(solution)/shard_map/ta,td->ad/dot_general | solution.py:87
  352.9 7.4 %fusion.61 = f32[1536,8,288]{0,2,1:T(8,128)} fusion(bf16[1,256,8,96]{1,3,2,0:T(8,128)(2,1)S(1)} %copy-done.18, bf16[1,256,8,96]{1,3,2,0:T(8,128)(2,1)S(1)} %copy-done.16, bf16[1,256,8,96]{1,3,2,0:T(8,128)(2,1)S(1)} %copy-done.24, bf16[256,1536]{1,0:T(8,128)(2,1)S(1)} %copy-done.1, f32[1536]{0:T(1024)S(1)} %copy-done.26, f32[256]{0:T(256)S(1)} %bitcast.201), kind=kOutput, calls=%fused_computation.87 | convolution fusion | flops 1817051136 | bytes 16129024 | tf_op jit(solution)/shard_map/td,tgc->dgc/dot_general | solution.py:91
  360.3 25.7 %all-reduce.26.cloned.1.call-done = (bf16[256,1536]{1,0:T(8,128)(2,1)}, bf16[256,1536]{1,0:T(8,128)(2,1)}) async-done(((bf16[256,1536]{1,0:T(8,128)(2,1)}, bf16[256,1536]{1,0:T(8,128)(2,1)}), (bf16[256,1536]{1,0:T(8,128)(2,1)}, bf16[256,1536]{1,0:T(8,128)(2,1)})) %all-reduce.26.cloned.1.call-update) | async-done | bytes 1572880 | tf_op jit(solution)/shard_map/psum | solution.py:103
  386.1 2.6 fusion.47
  388.7 4.9 %psum.95 = f32[256,1]{0,1:T(1,128)S(1)} all-reduce(f32[256,1]{0,1:T(1,128)S(1)} %bitcast.208), channel_id=1, replica_groups=mesh['dp'=1,'embed'=2,'heads'=4] {'embed'}, use_global_device_ids=true, to_apply=%region_18.19 | all-reduce | flops 256 | bytes 2048 | tf_op jit(solution)/shard_map/psum | solution.py:99
  393.6 3.1 fusion.41
  396.7 1.1 fusion.54
  (85 shorter events, 0.6 us)
Async XLA Ops:
  7.2 58.7 %copy-start = (bf16[768,1536]{1,0:T(8,128)(2,1)S(1)}, bf16[768,1536]{1,0:T(8,128)(2,1)}, u32[]{:S(2)}) copy-start(bf16[768,1536]{1,0:T(8,128)(2,1)} %param.14) | copy-start | bytes 7077892
  7.2 53.1 %all-reduce.18.cloned.1.call-start = ((), (), s32[]{:S(2)}) async-start(), calls=%async_computation | async-start | bytes 2359296 | tf_op jit(solution)/shard_map/psum | solution.py:99
  15.0 6.4 %copy-start.31 = (f32[256,1]{0,1:T(1,128)}, f32[256,1]{0,1:T(1,128)S(1)}, u32[]{:S(2)}) copy-start(f32[256,1]{0,1:T(1,128)S(1)} %add_rsqrt_fusion.1) | copy-start | bytes 3076
  15.0 6.5 %copy-start.33 = (s32[256]{0:T(256)S(1)}, s32[256]{0:T(256)}, u32[]{:S(2)}) copy-start(s32[256]{0:T(256)} %param.10) | copy-start | bytes 3076
  21.5 75.6 %all-reduce.20.cloned.1.call-start = ((), (), s32[]{:S(2)}) async-start(), calls=%async_computation.1 | async-start | bytes 1572864 | tf_op jit(solution)/shard_map/psum | solution.py:103
  21.6 42.1 %copy-start.21 = (pred[256,256]{0,1:T(8,128)(4,1)}, pred[256,256]{0,1:T(8,128)(4,1)S(1)}, u32[]{:S(2)}) copy-start(pred[256,256]{0,1:T(8,128)(4,1)S(1)} %iota_compare_fusion) | copy-start | bytes 196612
  22.0 40.9 %copy-start.6 = (f32[256,96]{0,1:T(8,128)}, f32[256,96]{0,1:T(8,128)S(1)}, u32[]{:S(2)}) copy-start(f32[256,96]{0,1:T(8,128)S(1)} %get-tuple-element.47) | copy-start | bytes 294916
  22.1 40.9 %copy-start.8 = (f32[256,96]{0,1:T(8,128)}, f32[256,96]{0,1:T(8,128)S(1)}, u32[]{:S(2)}) copy-start(f32[256,96]{0,1:T(8,128)S(1)} %get-tuple-element.48) | copy-start | bytes 294916
  61.6 1.3 copy-start.10
  63.0 0.8 copy-start.11
  63.1 1.0 copy-start.13
  63.7 2.1 copy-start.2
  64.2 1.7 copy-start.27
  65.9 1.8 copy-start.5
  67.6 133.3 %all-reduce.28.cloned.1.call-start = ((), (), s32[]{:S(2)}) async-start(), calls=%async_computation.5 | async-start | bytes 6291456 | tf_op jit(solution)/shard_map/psum | solution.py:99
  73.2 33.2 %copy-start.25 = (f32[1536]{0:T(1024)S(1)}, f32[1536]{0:T(1024)}, u32[]{:S(2)}) copy-start(f32[1536]{0:T(1024)} %param.12) | copy-start | bytes 18436
  105.8 0.6 copy-start.29
  120.7 180.3 %all-reduce.22.cloned.1.call-start = ((), (), s32[]{:S(2)}) async-start(), calls=%async_computation.2 | async-start | bytes 1572864 | tf_op jit(solution)/shard_map/psum | solution.py:103
  200.8 2.2 copy-start.19
  203.1 2.3 copy-start.30
  271.4 64.7 %all-reduce.24.cloned.1.call-start = ((), (), s32[]{:S(2)}) async-start(), calls=%async_computation.3 | async-start | bytes 786432 | tf_op jit(solution)/shard_map/psum | solution.py:99
  311.6 0.9 copy-start.4
  316.0 70.1 %all-reduce.26.cloned.1.call-start = ((), (), s32[]{:S(2)}) async-start(), calls=%async_computation.4 | async-start | bytes 3145728 | tf_op jit(solution)/shard_map/psum | solution.py:103
  321.8 17.2 %copy-start.28 = (f32[8,256]{1,0:T(8,128)S(1)}, f32[8,256]{1,0:T(8,128)}, u32[]{:S(2)}) copy-start(f32[8,256]{1,0:T(8,128)} %copy-done.27) | copy-start | bytes 24580
  336.2 2.9 copy-start.3
  336.2 2.9 copy-start.12
  336.2 2.9 copy-start.22
  339.0 1.1 copy-start.14
  340.1 1.1 copy-start.9
  341.2 0.9 copy-start.7
  341.4 1.1 copy-start.34
  342.1 2.6 slice-start
  342.3 0.9 copy-start.15
  342.5 0.7 copy-start.17
  342.5 3.1 slice-start.1
  343.3 0.8 copy-start.23
  348.6 4.3 %copy-start.1 = (bf16[256,1536]{1,0:T(8,128)(2,1)S(1)}, bf16[256,1536]{1,0:T(8,128)(2,1)}, u32[]{:S(2)}) copy-start(bf16[256,1536]{1,0:T(8,128)(2,1)} %param.9) | copy-start | bytes 2359300
  348.6 4.3 %copy-start.16 = (bf16[1,256,8,96]{1,3,2,0:T(8,128)(2,1)S(1)}, bf16[1,256,8,96]{1,3,2,0:T(8,128)(2,1)}, u32[]{:S(2)}) copy-start(bf16[1,256,8,96]{1,3,2,0:T(8,128)(2,1)} %copy-done.15) | copy-start | bytes 1179652
  348.6 4.3 %copy-start.18 = (bf16[1,256,8,96]{1,3,2,0:T(8,128)(2,1)S(1)}, bf16[1,256,8,96]{1,3,2,0:T(8,128)(2,1)}, u32[]{:S(2)}) copy-start(bf16[1,256,8,96]{1,3,2,0:T(8,128)(2,1)} %copy-done.17) | copy-start | bytes 1179652
  348.6 4.3 %copy-start.24 = (bf16[1,256,8,96]{1,3,2,0:T(8,128)(2,1)S(1)}, bf16[1,256,8,96]{1,3,2,0:T(8,128)(2,1)}, u32[]{:S(2)}) copy-start(bf16[1,256,8,96]{1,3,2,0:T(8,128)(2,1)} %copy-done.23) | copy-start | bytes 1179652
  348.6 4.3 %copy-start.26 = (f32[1536]{0:T(1024)S(1)}, f32[1536]{0:T(1024)}, u32[]{:S(2)}) copy-start(f32[1536]{0:T(1024)} %param.11) | copy-start | bytes 18436
  348.6 4.3 %copy-start.32 = (f32[256,1]{0,1:T(1,128)S(1)}, f32[256,1]{0,1:T(1,128)}, u32[]{:S(2)}) copy-start(f32[256,1]{0,1:T(1,128)} %copy-done.31) | copy-start | bytes 3076
  393.6 3.1 copy-start.20
Sparse Core Ops, SparseCore 0:
  21.6 38.6 all-reduce.17
  67.7 29.3 all-reduce.19
  120.8 79.9 all-reduce.27
  271.6 29.3 all-reduce.21
  316.1 19.9 all-reduce.23
  348.7 37.3 all-reduce.25
where the time goes:
time: 411 us; the launch traced here: 405 us
  waiting for transfers between devices  202 us (49%)
  matrix products  90 us (22%)
  local copies, waits for them, and re-layouts  49.6 us (12%)
  other arithmetic  25.2 us (6%)
  blocking collectives  22.5 us (5%)
  between operations  15.1 us (4%)
    psum x3, waiting for transfers between devices, sum_over_embed(): return lax.psum(partial_sum, 'embed')  131 us
    psum x3, waiting for transfers between devices, sum_over_heads(): return lax.psum(partial_sum, 'heads')  70.8 us
    unnamed x75, local copies, waits for them, and re-layouts  47.7 us
    psum x4, blocking collectives, sum_over_embed(): return lax.psum(partial_sum, 'embed')  22.5 us
    dot_general x1, matrix products, layer_step(): jnp.einsum('td,dkf->tkf', normed_two, w_gu, preferred_element_type=jnp.fl...  14.3 us
    dot_general x1, matrix products, layer_step(): jnp.einsum('tkf,dkf->td', grad_gate_up, w_gu, preferred_element_type=jnp....  13.8 us
    dot_general x1, matrix products, layer_step(): jnp.einsum('td,tkf->dkf', normed_two, grad_gate_up, preferred_element_typ...  10.5 us
  transfers between devices with their start and end apart: 6, of which 6 were waited for; matrix products, arithmetic and copies ran while one was open for 8% of the time, Pallas kernels for 0%

commit v1 on v0

v1 whole, which is shorter than its diff:
```python
import functools

import jax
import jax.numpy as jnp
from jax import lax
from jax.experimental import pallas as pl
from jax.experimental.pallas import tpu as pltpu
from jax.sharding import PartitionSpec as P

EPSILON = 1e-5
ROPE_BASE = 10000.0
HEAD = 96
HALF = HEAD // 2
GROUP = 3 * HEAD
CHUNKS = 2
MESH = pl.DeviceIdType.MESH
BF = jnp.bfloat16
F32 = jnp.float32

AR_OUT, AR_R2, AR_Y, AR_R1 = range(4)


def dot_nn(lhs, rhs):
    return lax.dot_general(lhs, rhs, (((1,), (0,)), ((), ())), preferred_element_type=F32)


def dot_nt(lhs, rhs):
    return lax.dot_general(lhs, rhs, (((1,), (1,)), ((), ())), preferred_element_type=F32)


def dot_tn(lhs, rhs):
    return lax.dot_general(lhs, rhs, (((0,), (0,)), ((), ())), preferred_element_type=F32)


def add_bf(one, two):
    return (one.astype(F32) + two.astype(F32)).astype(BF)


def step(index, size):
    return pl.ds(pl.multiple_of(index * size, size), size)


def layer_kernel(x_hbm, dy_hbm, g1_ref, g2_ref, cos_ref, sin_ref, wqkv_hbm, wout_hbm, wgu_hbm, wdown_hbm,
                 y_hbm, dx_hbm, dg1_ref, dg2_ref, r1_hbm, dqkv_hbm, mix_hbm, dh_hbm, r2_hbm, dgu_hbm, act_hbm,
                 x_ref, dy_ref, wqkv_ref, wout_ref, wg_ref, wu_ref, wdown_ref, raw_ref,
                 r1_ref, r2_ref, h_ref, dh_ref, act_ref, dgu_ref, rot_ref, prob_ref, mix_ref, dqkv_ref, dx_ref,
                 inv1_ref, inv2_ref,
                 ga_send, ga_recv, qkv_send, qkv_recv, gu_send, gu_recv, gm_send, gm_recv, stat_send, stat_recv,
                 part_ref, sib_ref, half_ref, far_ref, full_ref,
                 load_sem, raw_sem, store_sem,
                 st_s, st_r, ga_s, ga_r, qk_s, qk_r, gu_s, gu_r, gm_s, gm_r, p1_s, p1_r, p2_s, p2_r, p3_s, p3_r):
    tokens, width = x_ref.shape
    full_width = 2 * width
    ff = wdown_ref.shape[0]
    heads = wqkv_ref.shape[0] // GROUP
    half_width = width // 2
    rows = tokens // CHUNKS
    emb = lax.axis_index("embed")
    hid = lax.axis_index("heads")
    core = lax.rem(hid, 2)
    sibling = {"heads": hid + 1 - 2 * core}
    across = {"heads": lax.rem(hid + 2, 4)}
    partner = {"embed": 1 - emb}

    barrier = pltpu.get_barrier_semaphore()
    for peer in (sibling, across, partner):
        pl.semaphore_signal(barrier, inc=1, device_id=peer, device_id_type=MESH)

    def load(src, dst, sem):
        return pltpu.make_async_copy(src, dst, load_sem.at[sem])

    loads = [load(x_hbm, x_ref, 0), load(dy_hbm, dy_ref, 1), load(wdown_hbm, wdown_ref, 2),
             load(wqkv_hbm, wqkv_ref, 3), load(wout_hbm, wout_ref, 4)]
    for copy in loads[:3]:
        copy.start()

    raw_rows = raw_ref.shape[1]
    raw_steps = wgu_hbm.shape[0] // raw_rows

    def raw_load(index, slot):
        return pltpu.make_async_copy(wgu_hbm.at[step(index, raw_rows)], raw_ref.at[slot], raw_sem.at[slot])

    def store(src, dst, sem):
        copy = pltpu.make_async_copy(src, dst, store_sem.at[sem])
        copy.start()
        return copy

    def send(src, dst, s_sem, r_sem, peer):
        return pltpu.make_async_remote_copy(src_ref=src, dst_ref=dst, send_sem=s_sem, recv_sem=r_sem,
                                            device_id=peer, device_id_type=MESH)

    def stat_copy(k):
        return send(stat_send.at[k], stat_recv.at[k], st_s.at[k], st_r.at[k], partner)

    ga_cols = ff // 8

    def ga_copy(k):
        cols = step(k, ga_cols)
        return send(ga_send.at[:, cols], ga_recv.at[:, cols], ga_s.at[k], ga_r.at[k], partner)

    def qkv_copy(j):
        r = step(j, GROUP)
        return send(qkv_send.at[r], qkv_recv.at[r], qk_s.at[j], qk_r.at[j], partner)

    gu_cols = ff // 2

    def gu_copy(c, p):
        col = (p % 2) * ff + (p // 2) * gu_cols
        at = (pl.ds(c * rows, rows), pl.ds(col, gu_cols))
        return send(gu_send.at[at], gu_recv.at[at], gu_s.at[4 * c + p], gu_r.at[4 * c + p], partner)

    def gm_copy(c):
        at = (slice(None), pl.ds(c * rows, rows))
        return send(gm_send.at[at], gm_recv.at[at], gm_s.at[c], gm_r.at[c], partner)

    own = pl.ds(pl.multiple_of(core * half_width, half_width), half_width)
    other = pl.ds(pl.multiple_of((1 - core) * half_width, half_width), half_width)

    def p1_copy(i, c):
        r = pl.ds(c * rows, rows)
        k = i * CHUNKS + c
        return send(part_ref.at[i, r, other], sib_ref.at[i, r], p1_s.at[k], p1_r.at[k], sibling)

    def p2_copy(i, c):
        r = pl.ds(c * rows, rows)
        k = i * CHUNKS + c
        return send(half_ref.at[i, r], far_ref.at[i, r], p2_s.at[k], p2_r.at[k], across)

    def p3_copy(i, c):
        r = pl.ds(c * rows, rows)
        k = i * CHUNKS + c
        return send(full_ref.at[i, r, own], full_ref.at[i, r, own], p3_s.at[k], p3_r.at[k], sibling)

    def stage2(i, c):
        r = pl.ds(c * rows, rows)
        p1_copy(i, c).wait_recv()
        half_ref[i, r, :] = add_bf(part_ref[i, r, own], sib_ref[i, r, :])
        p2_copy(i, c).start()

    def stage3(i, c):
        r = pl.ds(c * rows, rows)
        p2_copy(i, c).wait_recv()
        full_ref[i, r, own] = add_bf(half_ref[i, r, :], far_ref[i, r, :])
        p3_copy(i, c).start()

    def stage4(i, c):
        p3_copy(i, c).wait_recv()

    def stat_put(k, col, n):
        flat = jnp.broadcast_to(col, (n, 128)).T[0:8, :]
        stat_send[k, :, 0:n] = flat
        stat_copy(k).start()

    def stat_get(k, n):
        stat_copy(k).wait_recv()
        total = stat_send[k, 0:1, 0:n] + stat_recv[k, 0:1, 0:n]
        return jnp.broadcast_to(total, (128, n)).T[:, 0:1]

    loads[0].wait()
    x32 = x_ref[...].astype(F32)
    sq1 = jnp.sum(x32 * x32, axis=-1, keepdims=True)
    pl.semaphore_wait(barrier, 3)
    stat_put(0, sq1, tokens)
    for copy in loads[3:]:
        copy.start()
    for slot in range(2):
        raw_load(slot, slot).start()

    loads[1].wait()
    loads[2].wait()

    def ga_body(k, carry):
        cols = step(k, ga_cols)
        ga_send[:, cols] = dot_nt(dy_ref[...], wdown_ref[cols, :]).astype(BF)

        @pl.when(k == 0)
        def _():
            ga_copy(k).start()
        return carry

    lax.fori_loop(0, 8, ga_body, 0)

    inv1 = lax.rsqrt(stat_get(0, tokens) / full_width + EPSILON)
    inv1_ref[...] = inv1
    r1_ref[...] = (x_ref[...].astype(F32) * inv1 * g1_ref[...]).astype(BF)
    stores = [store(r1_ref, r1_hbm, 0)]

    loads[3].wait()

    def qkv_body(j, carry):
        r = step(j, GROUP)
        qkv_send[r, :] = dot_nt(wqkv_ref[r, :], r1_ref[...]).astype(BF)
        qkv_copy(j).start()
        return carry

    lax.fori_loop(0, heads, qkv_body, 0)
    for k in range(1, 5):
        ga_copy(k).start()

    row_i = lax.broadcasted_iota(jnp.int32, (256, 256), 0)
    col_i = lax.broadcasted_iota(jnp.int32, (256, 256), 1)
    perm = (col_i == (row_i % 8) * 32 + row_i // 8).astype(F32).astype(BF)
    blocks = raw_rows // 512

    def raw_body(i, carry):
        slot = lax.rem(i, 2)
        raw_load(i, slot).wait()

        def block_body(b, inner):
            for u in range(4):
                base = pl.multiple_of(b * 2048 + u * 512, 512)
                pair = jnp.concatenate([raw_ref[slot, pl.ds(base, 256), :], raw_ref[slot, pl.ds(base + 256, 256), :]], axis=1)
                out = dot_nn(perm, pair)
                d = pl.ds(pl.multiple_of(i * (raw_rows // 32) + b * 64 + u * 16, 16), 16)
                for t in range(16):
                    for k, dst in ((0, wg_ref), (1, wu_ref)):
                        r = (2 * t + k) * 8
                        both = jnp.concatenate([out[r:r + 8, 0:128], out[r:r + 8, 128:256]], axis=0)
                        dst[d, t * 128:(t + 1) * 128] = both.astype(BF)
            return inner

        lax.fori_loop(0, blocks // 4, block_body, 0)

        @pl.when(i + 2 < raw_steps)
        def _():
            raw_load(i + 2, slot).start()
        return carry

    lax.fori_loop(0, raw_steps, raw_body, 0)

    scale = HEAD ** -0.5
    causal = (lax.broadcasted_iota(jnp.int32, (tokens, tokens), 0) <= lax.broadcasted_iota(jnp.int32, (tokens, tokens), 1))

    def rope(v, cos_t, sin_t):
        v = v.astype(F32)
        one, two = v[0:HALF], v[HALF:HEAD]
        return jnp.concatenate([one * cos_t - two * sin_t, two * cos_t + one * sin_t], axis=0).astype(BF)

    def unrope(v, cos_t, sin_t):
        v = v.astype(F32)
        one, two = v[0:HALF], v[HALF:HEAD]
        return jnp.concatenate([one * cos_t + two * sin_t, two * cos_t - one * sin_t], axis=0).astype(BF)

    def attn_body(j, carry):
        qkv_copy(j).wait_recv()
        base = pl.multiple_of(j * GROUP, 32)
        r_q, r_k, r_v = (pl.ds(base + n * HEAD, HEAD) for n in range(3))
        cos_t, sin_t = cos_ref[...], sin_ref[...]
        q = rope(add_bf(qkv_send[r_q, :], qkv_recv[r_q, :]), cos_t, sin_t)
        k = rope(add_bf(qkv_send[r_k, :], qkv_recv[r_k, :]), cos_t, sin_t)
        v = add_bf(qkv_send[r_v, :], qkv_recv[r_v, :])
        rot_ref[r_q, :] = q
        rot_ref[r_k, :] = k
        rot_ref[r_v, :] = v
        scores = jnp.where(causal, dot_tn(k, q) * scale, -1e30)
        weight = jnp.exp(scores - jnp.max(scores, axis=0, keepdims=True))
        prob = weight / jnp.sum(weight, axis=0, keepdims=True)
        prob_ref[j] = prob
        mix_ref[pl.ds(pl.multiple_of(j * HEAD, 32), HEAD), :] = dot_nn(v, prob.astype(BF)).astype(BF)
        return carry

    lax.fori_loop(0, heads, attn_body, 0)
    stores.append(store(mix_ref, mix_hbm, 1))

    loads[4].wait()
    for c in range(CHUNKS):
        r = pl.ds(c * rows, rows)
        part_ref[AR_OUT, r, :] = dot_tn(mix_ref[:, c * rows:(c + 1) * rows], wout_ref[...]).astype(BF)
        p1_copy(AR_OUT, c).start()
    for c in range(CHUNKS):
        stage2(AR_OUT, c)
    for c in range(CHUNKS):
        stage3(AR_OUT, c)
    for c in range(CHUNKS):
        r = pl.ds(c * rows, rows)
        stage4(AR_OUT, c)
        h = add_bf(x_ref[r, :], full_ref[AR_OUT, r, :])
        h_ref[r, :] = h
        h32 = h.astype(F32)
        stat_put(1 + c, jnp.sum(h32 * h32, axis=-1, keepdims=True), rows)
    for k in range(5, 8):
        ga_copy(k).start()

    tile = 512
    for c in range(CHUNKS):
        r = pl.ds(c * rows, rows)
        inv2 = lax.rsqrt(stat_get(1 + c, rows) / full_width + EPSILON)
        inv2_ref[r, :] = inv2
        r2 = (h_ref[r, :].astype(F32) * inv2 * g2_ref[...]).astype(BF)
        r2_ref[r, :] = r2
        for p in range(4):
            w_ref = (wg_ref, wu_ref)[p % 2]

            def gu_body(n, carry, c=c, p=p, w_ref=w_ref):
                src = pl.ds(pl.multiple_of((p // 2) * gu_cols + n * tile, tile), tile)
                dst = pl.ds(pl.multiple_of((p % 2) * ff + (p // 2) * gu_cols + n * tile, tile), tile)
                gu_send[pl.ds(c * rows, rows), dst] = dot_nn(r2_ref[pl.ds(c * rows, rows), :], w_ref[:, src]).astype(BF)
                return carry

            lax.fori_loop(0, gu_cols // tile, gu_body, 0)
            gu_copy(c, p).start()
    stores.append(store(r2_ref, r2_hbm, 2))

    for k in range(8):
        ga_copy(k).wait_recv()

    def mlp_chunk(c):
        r = pl.ds(c * rows, rows)
        for hf in range(2):
            gu_copy(c, 2 * hf).wait_recv()
            gu_copy(c, 2 * hf + 1).wait_recv()

            def act_body(n, carry, hf=hf):
                cg = pl.ds(pl.multiple_of(hf * gu_cols + n * 256, 256), 256)
                cu = pl.ds(pl.multiple_of(ff + hf * gu_cols + n * 256, 256), 256)
                gate = add_bf(gu_send[r, cg], gu_recv[r, cg]).astype(F32)
                up = add_bf(gu_send[r, cu], gu_recv[r, cu]).astype(F32)
                ga = add_bf(ga_send[r, cg], ga_recv[r, cg]).astype(F32)
                sig = 1.0 / (1.0 + jnp.exp(-gate))
                silu = gate * sig
                act_ref[r, cg] = (silu * up).astype(BF)
                dgu_ref[r, cg] = (ga * up * (sig * (1.0 + gate * (1.0 - sig)))).astype(BF)
                dgu_ref[r, cu] = (ga * silu).astype(BF)
                return carry

            lax.fori_loop(0, gu_cols // 256, act_body, 0)

        def r2_body(n, carry):
            w = step(n, tile)
            part_ref[AR_R2, r, w] = (dot_nt(dgu_ref[r, 0:ff], wg_ref[w, :]) + dot_nt(dgu_ref[r, ff:2 * ff], wu_ref[w, :])).astype(BF)
            return carry

        lax.fori_loop(0, width // tile, r2_body, 0)
        p1_copy(AR_R2, c).start()

    def down_chunk(c):
        r = pl.ds(c * rows, rows)

        def down_body(n, carry):
            w = step(n, tile)
            part_ref[AR_Y, r, w] = dot_nn(act_ref[r, :], wdown_ref[:, w]).astype(BF)
            return carry

        lax.fori_loop(0, width // tile, down_body, 0)
        p1_copy(AR_Y, c).start()

    dg2_ref[...] = jnp.zeros_like(dg2_ref)

    def norm2_back(c):
        r = pl.ds(c * rows, rows)
        stage4(AR_R2, c)
        gin = full_ref[AR_R2, r, :].astype(F32)
        unit = h_ref[r, :].astype(F32) * inv2_ref[r, :]
        dg2_ref[...] += jnp.sum(gin * unit, axis=0, keepdims=True)
        stat_put(3 + c, jnp.sum(gin * g2_ref[...] * unit, axis=-1, keepdims=True), rows)

    def hidden_back(c):
        r = pl.ds(c * rows, rows)
        dots = stat_get(3 + c, rows)
        inv2 = inv2_ref[r, :]
        unit = h_ref[r, :].astype(F32) * inv2
        scaled = full_ref[AR_R2, r, :].astype(F32) * g2_ref[...]
        norm = inv2 * (scaled - unit * (dots / full_width))
        dh_ref[r, :] = (dy_ref[r, :].astype(F32) + norm).astype(BF)
        gm_send[:, c * rows:(c + 1) * rows] = dot_nt(wout_ref[...], dh_ref[r, :]).astype(BF)
        gm_copy(c).start()

    def y_chunk(c):
        r = pl.ds(c * rows, rows)
        stage4(AR_Y, c)
        h_ref[r, :] = add_bf(h_ref[r, :], full_ref[AR_Y, r, :])

    mlp_chunk(0)
    down_chunk(0)
    stage2(AR_R2, 0)
    stage3(AR_R2, 0)
    stage2(AR_Y, 0)
    norm2_back(0)
    stage3(AR_Y, 0)
    mlp_chunk(1)
    stores.append(store(dgu_ref, dgu_hbm, 3))
    stores.append(store(act_ref, act_hbm, 4))
    stage2(AR_R2, 1)
    hidden_back(0)
    stage3(AR_R2, 1)
    norm2_back(1)
    down_chunk(1)
    hidden_back(1)
    stores.append(store(dh_ref, dh_hbm, 5))
    stage2(AR_Y, 1)
    y_chunk(0)
    stage3(AR_Y, 1)
    y_chunk(1)
    stores.append(store(h_ref, y_hbm, 6))

    for c in range(CHUNKS):
        gm_copy(c).wait_recv()

    def back_body(j, carry):
        base = pl.multiple_of(j * GROUP, 32)
        r_q, r_k, r_v = (pl.ds(base + n * HEAD, HEAD) for n in range(3))
        r_a = pl.ds(pl.multiple_of(j * HEAD, 32), HEAD)
        cos_t, sin_t = cos_ref[...], sin_ref[...]
        da = add_bf(gm_send[r_a, :], gm_recv[r_a, :])
        q, k, v = rot_ref[r_q, :], rot_ref[r_k, :], rot_ref[r_v, :]
        prob = prob_ref[j]
        dp = dot_tn(v, da).astype(BF).astype(F32)
        dqkv_ref[r_v, :] = dot_nt(da, prob.astype(BF)).astype(BF)
        weighted = prob * dp
        ds = ((weighted - prob * jnp.sum(weighted, axis=0, keepdims=True)) * scale).astype(BF)
        dqkv_ref[r_q, :] = unrope(dot_nn(k, ds).astype(BF), cos_t, sin_t)
        dqkv_ref[r_k, :] = unrope(dot_nt(q, ds).astype(BF), cos_t, sin_t)
        return carry

    lax.fori_loop(0, heads, back_body, 0)
    stores.append(store(dqkv_ref, dqkv_hbm, 7))

    for c in range(CHUNKS):
        r = pl.ds(c * rows, rows)
        part_ref[AR_R1, r, :] = dot_tn(dqkv_ref[:, c * rows:(c + 1) * rows], wqkv_ref[...]).astype(BF)
        p1_copy(AR_R1, c).start()
    for c in range(CHUNKS):
        stage2(AR_R1, c)
    for c in range(CHUNKS):
        stage3(AR_R1, c)
    dg1_ref[...] = jnp.zeros_like(dg1_ref)
    for c in range(CHUNKS):
        r = pl.ds(c * rows, rows)
        stage4(AR_R1, c)
        gin = full_ref[AR_R1, r, :].astype(F32)
        unit = x_ref[r, :].astype(F32) * inv1_ref[r, :]
        dg1_ref[...] += jnp.sum(gin * unit, axis=0, keepdims=True)
        stat_put(5 + c, jnp.sum(gin * g1_ref[...] * unit, axis=-1, keepdims=True), rows)
    for c in range(CHUNKS):
        r = pl.ds(c * rows, rows)
        dots = stat_get(5 + c, rows)
        inv1 = inv1_ref[r, :]
        unit = x_ref[r, :].astype(F32) * inv1
        scaled = full_ref[AR_R1, r, :].astype(F32) * g1_ref[...]
        norm = inv1 * (scaled - unit * (dots / full_width))
        dx_ref[r, :] = (dh_ref[r, :].astype(F32) + norm).astype(BF)
    stores.append(store(dx_ref, dx_hbm, 8))

    for k in range(7):
        stat_copy(k).wait_send()
    for k in range(8):
        ga_copy(k).wait_send()
    for j in range(heads):
        qkv_copy(j).wait_send()
    for c in range(CHUNKS):
        for p in range(4):
            gu_copy(c, p).wait_send()
        gm_copy(c).wait_send()
        for i in range(4):
            p1_copy(i, c).wait_send()
            p2_copy(i, c).wait_send()
            p3_copy(i, c).wait_send()
    for copy in stores:
        copy.wait()


def run_layer(x_in, cos_t, sin_t, gain_one, gain_two, w_qkv, w_out, w_gu, w_down, grad_out):
    tokens, width = x_in.shape
    ff = w_down.shape[0]
    chans = w_qkv.shape[0]
    mix = w_out.shape[0]
    heads = mix // HEAD
    rows = tokens // CHUNKS
    act = lambda n, dtype=BF: jax.ShapeDtypeStruct((tokens, n), dtype)
    any_spec = pl.BlockSpec(memory_space=pl.ANY)
    vmem_spec = pl.BlockSpec(memory_space=pltpu.VMEM)
    raw_rows = 128 * 32
    scratch = [
        pltpu.VMEM((tokens, width), BF), pltpu.VMEM((tokens, width), BF),
        pltpu.VMEM((chans, width), BF), pltpu.VMEM((mix, width), BF),
        pltpu.VMEM((width, ff), BF), pltpu.VMEM((width, ff), BF), pltpu.VMEM((ff, width), BF),
        pltpu.VMEM((2, raw_rows, 128), BF),
        pltpu.VMEM((tokens, width), BF), pltpu.VMEM((tokens, width), BF), pltpu.VMEM((tokens, width), BF), pltpu.VMEM((tokens, width), BF),
        pltpu.VMEM((tokens, ff), BF), pltpu.VMEM((tokens, 2 * ff), BF),
        pltpu.VMEM((chans, tokens), BF), pltpu.VMEM((heads, tokens, tokens), F32), pltpu.VMEM((mix, tokens), BF), pltpu.VMEM((chans, tokens), BF),
        pltpu.VMEM((tokens, width), BF),
        pltpu.VMEM((tokens, 1), F32), pltpu.VMEM((tokens, 1), F32),
        pltpu.VMEM((tokens, ff), BF), pltpu.VMEM((tokens, ff), BF),
        pltpu.VMEM((chans, tokens), BF), pltpu.VMEM((chans, tokens), BF),
        pltpu.VMEM((tokens, 2 * ff), BF), pltpu.VMEM((tokens, 2 * ff), BF),
        pltpu.VMEM((mix, tokens), BF), pltpu.VMEM((mix, tokens), BF),
        pltpu.VMEM((7, 8, tokens), F32), pltpu.VMEM((7, 8, tokens), F32),
        pltpu.VMEM((4, tokens, width), BF), pltpu.VMEM((4, tokens, width // 2), BF), pltpu.VMEM((4, tokens, width // 2), BF),
        pltpu.VMEM((4, tokens, width // 2), BF), pltpu.VMEM((4, tokens, width), BF),
        pltpu.SemaphoreType.DMA((5,)), pltpu.SemaphoreType.DMA((2,)), pltpu.SemaphoreType.DMA((9,)),
    ]
    for n in (7, 8, heads, 4 * CHUNKS, CHUNKS, 4 * CHUNKS, 4 * CHUNKS, 4 * CHUNKS):
        scratch += [pltpu.SemaphoreType.DMA((n,)), pltpu.SemaphoreType.DMA((n,))]
    vec = jax.ShapeDtypeStruct((1, width), F32)
    return pl.pallas_call(
        layer_kernel,
        name="layer",
        out_shape=(act(width), act(width), vec, vec, act(width), jax.ShapeDtypeStruct((chans, tokens), BF),
                   jax.ShapeDtypeStruct((mix, tokens), BF), act(width), act(width), act(2 * ff), act(ff)),
        in_specs=[any_spec, any_spec, vmem_spec, vmem_spec, vmem_spec, vmem_spec, any_spec, any_spec, any_spec, any_spec],
        out_specs=(any_spec, any_spec, vmem_spec, vmem_spec) + (any_spec,) * 7,
        scratch_shapes=scratch,
        compiler_params=pltpu.CompilerParams(collective_id=0, has_side_effects=True, vmem_limit_bytes=67000000),
    )(x_in, grad_out, gain_one, gain_two, cos_t, sin_t, w_qkv, w_out, w_gu, w_down)


def product_call(lhs, rhs, block, transposed):
    n = lhs.shape[1] if transposed else lhs.shape[0]
    tokens, width = rhs.shape

    def body(lhs_ref, rhs_ref, out_ref):
        out_ref[...] = (dot_tn if transposed else dot_nn)(lhs_ref[...], rhs_ref[...])

    lhs_spec = pl.BlockSpec((tokens, block), lambda i: (0, i)) if transposed else pl.BlockSpec((block, tokens), lambda i: (i, 0))
    return pl.pallas_call(
        body,
        grid=(n // block,),
        in_specs=[lhs_spec, pl.BlockSpec((tokens, width), lambda i: (0, 0))],
        out_specs=pl.BlockSpec((block, width), lambda i: (i, 0)),
        out_shape=jax.ShapeDtypeStruct((n, width), F32),
    )(lhs, rhs)


def gate_up_grad(r2, dgu):
    tokens, width = r2.shape
    ff = dgu.shape[1] // 2
    block = 128
    pad = 40
    steps = width // block

    def body(r2_ref, dgu_ref, out_hbm, stage_ref, sem):
        i = pl.program_id(0)
        slot = lax.rem(i, 2)

        def out_copy(index, s):
            return pltpu.make_async_copy(stage_ref.at[s, :, 0:32, :], out_hbm.at[pl.ds(index * block, block)], sem.at[s])

        @pl.when(i >= 2)
        def _():
            out_copy(i - 2, slot).wait()

        lhs = r2_ref[...].T
        for k in range(2):
            for n in range(ff // 512):
                val = dot_nn(lhs, dgu_ref[:, k * ff + n * 512:k * ff + (n + 1) * 512])
                for t in range(4):
                    row = 2 * (4 * n + t) + k
                    stage_ref[slot, :, row, :] = val[:, t * 128:(t + 1) * 128]
        out_copy(i, slot).start()

        @pl.when(i == steps - 1)
        def _():
            out_copy(i - 1, 1 - slot).wait()
            out_copy(i, slot).wait()

    out = pl.pallas_call(
        body,
        grid=(steps,),
        in_specs=[pl.BlockSpec((tokens, 128), lambda i: (0, i)) if block == 128 else pl.BlockSpec((None, tokens, block), lambda i: (i, 0, 0)),
                  pl.BlockSpec((tokens, 2 * ff), lambda i: (0, 0))],
        out_specs=pl.BlockSpec(memory_space=pl.ANY),
        out_shape=jax.ShapeDtypeStruct((width, 32, 128), F32),
        scratch_shapes=[pltpu.VMEM((2, block, pad, 128), F32), pltpu.SemaphoreType.DMA((2,))],
        compiler_params=pltpu.CompilerParams(vmem_limit_bytes=48 << 20),
    )(r2 if block == 128 else r2.reshape(tokens, steps, block).transpose(1, 0, 2), dgu)
    return out.reshape(width, 16, 2, 128).transpose(0, 2, 1, 3).reshape(width, 2, ff)


def rope_tables(positions):
    inv_freq = ROPE_BASE ** (-jnp.arange(0, HEAD, 2, dtype=F32) / HEAD)
    angles = inv_freq[:, None] * positions.astype(F32)[None, :]
    return jnp.cos(angles), jnp.sin(angles)


def solution(mesh):
    def per_device(x_in, positions, gain_one, gain_two, w_qkv, w_out, w_gu, w_down, grad_out):
        width, groups, chans = w_qkv.shape
        ff = w_down.shape[0]
        cos_t, sin_t = rope_tables(positions)
        qkv_rows = w_qkv.transpose(1, 2, 0).reshape(groups * chans, width)
        gu_rows = w_gu.reshape(width, 2, ff // 128, 128).transpose(0, 2, 1, 3).reshape(width * 2 * (ff // 128), 128)
        y, dx, dg1, dg2, r1, dqkv, mix, dh, r2, dgu, act = run_layer(
            x_in, cos_t, sin_t, gain_one.reshape(1, width), gain_two.reshape(1, width), qkv_rows, w_out, gu_rows, w_down, grad_out)
        d_down = product_call(act, grad_out, 256, True)
        d_gu = gate_up_grad(r2, dgu)
        d_out = product_call(mix, dh, 256, False)
        d_qkv = product_call(dqkv, r1, 256, False).reshape(groups, chans, width).transpose(2, 0, 1)
        return y, dx, dg1.reshape(width), dg2.reshape(width), d_qkv, d_out, d_gu, d_down

    act_spec = P('dp', 'embed')
    in_specs = (act_spec, P('dp'), P('embed'), P('embed'), P('embed', 'heads', None), P('heads', 'embed'), P('embed', None, 'heads'), P('heads', 'embed'), act_spec)
    out_specs = (act_spec, act_spec, P(('dp', 'embed')), P(('dp', 'embed')), P(('dp', 'embed'), 'heads', None), P(('dp', 'heads'), 'embed'), P(('dp', 'embed'), None, 'heads'), P(('dp', 'heads'), 'embed'))
    return jax.shard_map(per_device, mesh=mesh, in_specs=in_specs, out_specs=out_specs, check_vma=False)
```

time: 411 us -> 208 us (0.51); the launches traced: 405 us -> 207 us
  waiting for transfers between devices: 202 us -> 0 us
  Pallas kernels: 0 us -> 197 us
  matrix products: 90 us -> 0 us
  local copies, waits for them, and re-layouts: 49.6 us -> 7.08 us
  blocking collectives: 22.5 us -> 0 us
  other arithmetic: 25.2 us -> 2.83 us
  between operations: 15.1 us -> 0.68 us
    psum x6 -> x0, waiting for transfers between devices: 202 us -> none  [the longest x3 131 us: sum_over_embed(): return lax.psum(partial_sum, 'embed')]
    pallas_call x0 -> x5, Pallas kernels: none -> 197 us  [the longest x1 155 us: run_layer(): pl.pallas_call(layer_kernel, name='layer', out_shape=(act(width), act(wid...]
    dot_general x18 -> x0, matrix products: 90 us -> none  [the longest x1 14.3 us: layer_step(): jnp.einsum('td,dkf->tkf', normed_two, w_gu, preferred_element_type=jnp.fl...]
    unnamed x75 -> x14, local copies, waits for them, and re-layouts: 47.7 us -> 4.49 us
    psum x4 -> x0, blocking collectives: 22.5 us -> none  [sum_over_embed(): return lax.psum(partial_sum, 'embed')]
    reduce_sum x5 -> x0, other arithmetic: 9.28 us -> none  [the longest x2 5.02 us: rms_backward(): grad_gain = jnp.sum(grad_in * unit_rows, axis=0)]
    convert_element_type x8 -> x1, other arithmetic: 9.86 us -> 0.68 us  [rope_tables(): angles = inv_freq[:, None] * positions.astype(F32)[None, :]]
  transfers between devices with their start and end apart: 6 -> 0, of which waited for: 6 -> 0; matrix products, arithmetic and copies ran while one was open for 8% -> 0% of each run, Pallas kernels for 0% -> 0%
where the time goes in v1:
time: 208 us; the launch traced here: 207 us
  Pallas kernels  197 us (95%)
  local copies, waits for them, and re-layouts  7.08 us (3%)
  other arithmetic  2.83 us (1%)
    pallas_call x1, Pallas kernels, run_layer(): pl.pallas_call(layer_kernel, name='layer', out_shape=(act(width), act(wid...  155 us
    pallas_call x3, Pallas kernels, product_call(): pl.pallas_call(body, grid=(n // block,), in_specs=[lhs_spec, pl.BlockSpec...  22.2 us
    pallas_call x1, Pallas kernels, gate_up_grad(): pl.pallas_call(body, grid=(steps,), in_specs=[pl.BlockSpec((tokens, 128),...  18.9 us
    unnamed x14, local copies, waits for them, and re-layouts  4.49 us

profile of v1, /device:TPU:0, one launch (start us, length us, event | category | flops | bytes accessed | tf_op | source)
XLA Modules:
  0.0 207.1 jit_solution(10248389627907715448)
XLA Ops:
  0.6 0.7 convert_element_type.3
  1.3 0.9 multiply_sine_fusion
  2.2 1.3 reshape.54.g1_ref
  3.5 1.3 reshape.55.g2_ref
  4.8 155.4 %layer.1 = (bf16[256,1536]{1,0:T(8,128)(2,1)}, bf16[256,1536]{1,0:T(8,128)(2,1)}, f32[1,1536]{1,0:T(1,128)}, f32[1,1536]{1,0:T(1,128)}, bf16[256,1536]{1,0:T(8,1...) custom-call(bf16[256,1536]{1,0:T(8,128)(2,1)} %x_hbm.1, ...), custom_call_target="tpu_custom_call" | custom-call | tf_op jit(solution)/shard_map/layer/pallas_call | solution.py:495
  160.2 0.0 copy-start
  160.2 1.6 copy-done
  161.8 0.0 copy-start.1
  161.8 1.1 copy-done.1
  163.0 18.9 %shard_map.154 = f32[1536,32,128]{2,1,0:T(8,128)} custom-call(bf16[256,1536]{1,0:T(8,128)(2,1)S(1)} %copy-done.1, bf16[256,4096]{1,0:T(8,128)(2,1)S(1)} %copy-done), custom_call_target="tpu_custom_call" | custom-call | tf_op jit(solution)/shard_map/pallas_call | solution.py:556
  181.9 9.4 %shard_map.152 = f32[2304,1536]{1,0:T(8,128)} custom-call(bf16[2304,256]{1,0:T(8,128)(2,1)} %get-tuple-element.23.lhs_ref, bf16[256,1536]{1,0:T(8,128)(2,1)} %get-tuple-element.24.rhs_ref), custom_call_target="tpu_custom_call" | custom-call | tf_op jit(solution)/shard_map/pallas_call | solution.py:515
  191.3 4.2 %shard_map.153 = f32[768,1536]{1,0:T(8,128)} custom-call(bf16[768,256]{1,0:T(8,128)(2,1)} %get-tuple-element.25.lhs_ref, bf16[256,1536]{1,0:T(8,128)(2,1)} %get-tuple-element.26.rhs_ref), custom_call_target="tpu_custom_call" | custom-call | tf_op jit(solution)/shard_map/pallas_call | solution.py:515
  195.5 0.0 copy-start.5
  195.5 0.0 copy-start.4
  195.5 0.0 copy-start.3
  195.5 0.0 copy-start.2
  195.5 8.6 %shard_map.155 = f32[2048,1536]{1,0:T(8,128)} custom-call(bf16[256,2048]{1,0:T(8,128)(2,1)} %get-tuple-element.29.lhs_ref, bf16[256,1536]{1,0:T(8,128)(2,1)} %rhs_ref.1), custom_call_target="tpu_custom_call" | custom-call | tf_op jit(solution)/shard_map/pallas_call | solution.py:515
  204.1 0.0 copy-done.5
  204.1 0.6 reduce
  204.7 0.0 copy-done.4
  204.7 0.6 reduce.1
  205.4 0.0 copy-done.3
  205.4 0.9 copy.21
  206.2 0.0 copy-done.2
  206.2 0.9 copy.22
  (1 shorter events, 0.0 us)
Async XLA Ops:
  160.2 1.6 copy-start
  161.8 1.1 copy-start.1
  195.5 8.6 %copy-start.5 = (f32[1,1536]{1,0:T(1,128)S(1)}, f32[1,1536]{1,0:T(1,128)}, u32[]{:S(2)}) copy-start(f32[1,1536]{1,0:T(1,128)} %get-tuple-element.21) | copy-start | bytes 18436
  195.5 9.2 %copy-start.4 = (f32[1,1536]{1,0:T(1,128)S(1)}, f32[1,1536]{1,0:T(1,128)}, u32[]{:S(2)}) copy-start(f32[1,1536]{1,0:T(1,128)} %get-tuple-element.22) | copy-start | bytes 18436
  195.5 9.8 %copy-start.3 = (bf16[256,1536]{1,0:T(8,128)(2,1)S(1)}, bf16[256,1536]{1,0:T(8,128)(2,1)}, u32[]{:S(2)}) copy-start(bf16[256,1536]{1,0:T(8,128)(2,1)} %get-tuple-element.40) | copy-start | bytes 2359300
  195.5 10.7 %copy-start.2 = (bf16[256,1536]{1,0:T(8,128)(2,1)S(1)}, bf16[256,1536]{1,0:T(8,128)(2,1)}, u32[]{:S(2)}) copy-start(bf16[256,1536]{1,0:T(8,128)(2,1)} %get-tuple-element.41) | copy-start | bytes 2359300

commit v2 on v1

--- a/solution.py
+++ b/solution.py
@@ -1,4 +1,4 @@
-import functools
+import math
 
 import jax
 import jax.numpy as jnp
@@ -40,10 +40,10 @@
     return pl.ds(pl.multiple_of(index * size, size), size)
 
 
-def layer_kernel(x_hbm, dy_hbm, g1_ref, g2_ref, cos_ref, sin_ref, wqkv_hbm, wout_hbm, wgu_hbm, wdown_hbm,
+def layer_kernel(x_hbm, dy_hbm, g1_in, g2_in, pos_in, wqkv_hbm, wout_hbm, wgu_hbm, wdown_hbm,
                  y_hbm, dx_hbm, dg1_ref, dg2_ref, r1_hbm, dqkv_hbm, mix_hbm, dh_hbm, r2_hbm, dgu_hbm, act_hbm,
                  x_ref, dy_ref, wqkv_ref, wout_ref, wg_ref, wu_ref, wdown_ref, raw_ref,
-                 r1_ref, r2_ref, h_ref, dh_ref, act_ref, dgu_ref, rot_ref, prob_ref, mix_ref, dqkv_ref, dx_ref,
+                 g1_ref, g2_ref, cos_ref, sin_ref, r1_ref, r2_ref, h_ref, dh_ref, act_ref, dgu_ref, rot_ref, prob_ref, mix_ref, dqkv_ref, dx_ref,
                  inv1_ref, inv2_ref,
                  ga_send, ga_recv, qkv_send, qkv_recv, gu_send, gu_recv, gm_send, gm_recv, stat_send, stat_recv,
                  part_ref, sib_ref, half_ref, far_ref, full_ref,
@@ -156,6 +156,8 @@
         total = stat_send[k, 0:1, 0:n] + stat_recv[k, 0:1, 0:n]
         return jnp.broadcast_to(total, (128, n)).T[:, 0:1]
 
+    g1_ref[...] = g1_in[...].reshape(1, width)
+    g2_ref[...] = g2_in[...].reshape(1, width)
     loads[0].wait()
     x32 = x_ref[...].astype(F32)
     sq1 = jnp.sum(x32 * x32, axis=-1, keepdims=True)
@@ -179,6 +181,12 @@
         return carry
 
     lax.fori_loop(0, 8, ga_body, 0)
+
+    place = pos_in[...].reshape(1, tokens).astype(F32)
+    pair_i = lax.broadcasted_iota(jnp.int32, (HALF, 1), 0).astype(F32)
+    angles = jnp.exp(pair_i * (-2.0 * math.log(ROPE_BASE) / HEAD)) * place
+    cos_ref[...] = jnp.cos(angles)
+    sin_ref[...] = jnp.sin(angles)
 
     inv1 = lax.rsqrt(stat_get(0, tokens) / full_width + EPSILON)
     inv1_ref[...] = inv1
@@ -459,7 +467,7 @@
         copy.wait()
 
 
-def run_layer(x_in, cos_t, sin_t, gain_one, gain_two, w_qkv, w_out, w_gu, w_down, grad_out):
+def run_layer(x_in, positions, gain_one, gain_two, w_qkv, w_out, w_gu, w_down, grad_out):
     tokens, width = x_in.shape
     ff = w_down.shape[0]
     chans = w_qkv.shape[0]
@@ -475,6 +483,7 @@
         pltpu.VMEM((chans, width), BF), pltpu.VMEM((mix, width), BF),
         pltpu.VMEM((width, ff), BF), pltpu.VMEM((width, ff), BF), pltpu.VMEM((ff, width), BF),
         pltpu.VMEM((2, raw_rows, 128), BF),
+        pltpu.VMEM((1, width), F32), pltpu.VMEM((1, width), F32), pltpu.VMEM((HALF, tokens), F32), pltpu.VMEM((HALF, tokens), F32),
         pltpu.VMEM((tokens, width), BF), pltpu.VMEM((tokens, width), BF), pltpu.VMEM((tokens, width), BF), pltpu.VMEM((tokens, width), BF),
         pltpu.VMEM((tokens, ff), BF), pltpu.VMEM((tokens, 2 * ff), BF),
         pltpu.VMEM((chans, tokens), BF), pltpu.VMEM((heads, tokens, tokens), F32), pltpu.VMEM((mix, tokens), BF), pltpu.VMEM((chans, tokens), BF),
@@ -497,95 +506,136 @@
         name="layer",
         out_shape=(act(width), act(width), vec, vec, act(width), jax.ShapeDtypeStruct((chans, tokens), BF),
                    jax.ShapeDtypeStruct((mix, tokens), BF), act(width), act(width), act(2 * ff), act(ff)),
-        in_specs=[any_spec, any_spec, vmem_spec, vmem_spec, vmem_spec, vmem_spec, any_spec, any_spec, any_spec, any_spec],
+        in_specs=[any_spec, any_spec, vmem_spec, vmem_spec, vmem_spec, any_spec, any_spec, any_spec, any_spec],
         out_specs=(any_spec, any_spec, vmem_spec, vmem_spec) + (any_spec,) * 7,
         scratch_shapes=scratch,
         compiler_params=pltpu.CompilerParams(collective_id=0, has_side_effects=True, vmem_limit_bytes=67000000),
-    )(x_in, grad_out, gain_one, gain_two, cos_t, sin_t, w_qkv, w_out, w_gu, w_down)
-
-
-def product_call(lhs, rhs, block, transposed):
-    n = lhs.shape[1] if transposed else lhs.shape[0]
-    tokens, width = rhs.shape
-
-    def body(lhs_ref, rhs_ref, out_ref):
-        out_ref[...] = (dot_tn if transposed else dot_nn)(lhs_ref[...], rhs_ref[...])
-
-    lhs_spec = pl.BlockSpec((tokens, block), lambda i: (0, i)) if transposed else pl.BlockSpec((block, tokens), lambda i: (i, 0))
-    return pl.pallas_call(
-        body,
-        grid=(n // block,),
-        in_specs=[lhs_spec, pl.BlockSpec((tokens, width), lambda i: (0, 0))],
-        out_specs=pl.BlockSpec((block, width), lambda i: (i, 0)),
-        out_shape=jax.ShapeDtypeStruct((n, width), F32),
-    )(lhs, rhs)
-
-
-def gate_up_grad(r2, dgu):
-    tokens, width = r2.shape
-    ff = dgu.shape[1] // 2
-    block = 128
-    pad = 40
-    steps = width // block
-
-    def body(r2_ref, dgu_ref, out_hbm, stage_ref, sem):
-        i = pl.program_id(0)
+    )(x_in, grad_out, gain_one, gain_two, positions, w_qkv, w_out, w_gu, w_down)
+
+
+def grads_kernel(act_hbm, dy_hbm, r2_hbm, dgu_hbm, mix_hbm, dh_hbm, dqkv_hbm, r1_hbm, y_in, dx_in, dg1_in, dg2_in,
+                 down_out, gu_out, wout_out, qkv_out, y_out, dx_out, dg1_out, dg2_out,
+                 act_ref, dy_ref, r2_ref, dgu_ref, mix_ref, dh_ref, dqkv_ref, r1_ref, y_ref, dx_ref, rows_ref, inter_ref,
+                 load_sem, rows_sem, inter_sem, end_sem):
+    block = rows_ref.shape[1]
+    pad = inter_ref.shape[1] // GU_BLOCK
+    ff = dgu_ref.shape[1] // 2
+    pairs = [(dqkv_hbm, dqkv_ref), (r1_hbm, r1_ref), (r2_hbm, r2_ref), (dgu_hbm, dgu_ref), (mix_hbm, mix_ref), (dh_hbm, dh_ref),
+             (act_hbm, act_ref), (dy_hbm, dy_ref), (y_in, y_ref), (dx_in, dx_ref)]
+    loads = [pltpu.make_async_copy(src, dst, load_sem.at[n]) for n, (src, dst) in enumerate(pairs)]
+    for copy in loads:
+        copy.start()
+    dg1_out[...] = dg1_in[...].reshape(dg1_out.shape)
+    dg2_out[...] = dg2_in[...].reshape(dg2_out.shape)
+
+    slots = rows_ref.shape[0]
+
+    def rows_copy(out, index, slot):
+        return pltpu.make_async_copy(rows_ref.at[slot], out.at[step(index, block)], rows_sem.at[slot])
+
+    def product(out, lhs_of, rhs_ref, first):
+        def body(i, carry):
+            slot = lax.rem(i + first, slots)
+
+            @pl.when(i + first >= slots)
+            def _():
+                rows_copy(out, 0, slot).wait()
+            rows_ref[slot] = lhs_of(i, rhs_ref)
+            rows_copy(out, i, slot).start()
+            return carry
+        count = out.shape[0] // block
+        lax.fori_loop(0, count, body, 0)
+        return first + count
+
+    def plain_rows(ref):
+        return lambda i, rhs_ref: dot_nn(ref[step(i, block), :], rhs_ref[...])
+
+    loads[0].wait()
+    loads[1].wait()
+    sent = product(qkv_out, plain_rows(dqkv_ref), r1_ref, 0)
+
+    loads[2].wait()
+    loads[3].wait()
+
+    def inter_copy(index, slot):
+        return pltpu.make_async_copy(inter_ref.at[slot].reshape(GU_BLOCK, pad, 128).at[:, 0:32, :],
+                                     gu_out.at[step(index, GU_BLOCK)], inter_sem.at[slot])
+
+    gu_steps = gu_out.shape[0] // GU_BLOCK
+
+    def gu_body(i, carry):
         slot = lax.rem(i, 2)
-
-        def out_copy(index, s):
-            return pltpu.make_async_copy(stage_ref.at[s, :, 0:32, :], out_hbm.at[pl.ds(index * block, block)], sem.at[s])
 
         @pl.when(i >= 2)
         def _():
-            out_copy(i - 2, slot).wait()
-
-        lhs = r2_ref[...].T
+            inter_copy(0, slot).wait()
+        lhs = r2_ref[:, step(i, GU_BLOCK)].T
         for k in range(2):
             for n in range(ff // 512):
                 val = dot_nn(lhs, dgu_ref[:, k * ff + n * 512:k * ff + (n + 1) * 512])
                 for t in range(4):
                     row = 2 * (4 * n + t) + k
-                    stage_ref[slot, :, row, :] = val[:, t * 128:(t + 1) * 128]
-        out_copy(i, slot).start()
-
-        @pl.when(i == steps - 1)
-        def _():
-            out_copy(i - 1, 1 - slot).wait()
-            out_copy(i, slot).wait()
-
-    out = pl.pallas_call(
-        body,
-        grid=(steps,),
-        in_specs=[pl.BlockSpec((tokens, 128), lambda i: (0, i)) if block == 128 else pl.BlockSpec((None, tokens, block), lambda i: (i, 0, 0)),
-                  pl.BlockSpec((tokens, 2 * ff), lambda i: (0, 0))],
-        out_specs=pl.BlockSpec(memory_space=pl.ANY),
-        out_shape=jax.ShapeDtypeStruct((width, 32, 128), F32),
-        scratch_shapes=[pltpu.VMEM((2, block, pad, 128), F32), pltpu.SemaphoreType.DMA((2,))],
-        compiler_params=pltpu.CompilerParams(vmem_limit_bytes=48 << 20),
-    )(r2 if block == 128 else r2.reshape(tokens, steps, block).transpose(1, 0, 2), dgu)
-    return out.reshape(width, 16, 2, 128).transpose(0, 2, 1, 3).reshape(width, 2, ff)
-
-
-def rope_tables(positions):
-    inv_freq = ROPE_BASE ** (-jnp.arange(0, HEAD, 2, dtype=F32) / HEAD)
-    angles = inv_freq[:, None] * positions.astype(F32)[None, :]
-    return jnp.cos(angles), jnp.sin(angles)
+                    inter_ref[slot, pl.ds(row, GU_BLOCK, stride=pad), :] = val[:, t * 128:(t + 1) * 128]
+        inter_copy(i, slot).start()
+        return carry
+
+    lax.fori_loop(0, gu_steps, gu_body, 0)
+
+    loads[4].wait()
+    loads[5].wait()
+    sent = product(wout_out, plain_rows(mix_ref), dh_ref, sent)
+    loads[6].wait()
+    loads[7].wait()
+    sent = product(down_out, lambda i, rhs_ref: dot_tn(act_ref[:, step(i, block)], rhs_ref[...]), dy_ref, sent)
+    loads[8].wait()
+    loads[9].wait()
+    ends = [pltpu.make_async_copy(y_ref, y_out, end_sem.at[0]), pltpu.make_async_copy(dx_ref, dx_out, end_sem.at[1])]
+    for copy in ends:
+        copy.start()
+    for slot in range(slots):
+        rows_copy(down_out, 0, slot).wait()
+    for slot in range(2):
+        inter_copy(0, slot).wait()
+    for copy in ends:
+        copy.wait()
+
+
+GU_BLOCK = 128
+
+
+def weight_grads(act, grad_out, r2, dgu, mix, dh, dqkv, r1, y, dx, dg1, dg2):
+    tokens, width = r2.shape
+    ff = act.shape[1]
+    any_spec = pl.BlockSpec(memory_space=pl.ANY)
+    vmem_spec = pl.BlockSpec(memory_space=pltpu.VMEM)
+    out = lambda *shape: jax.ShapeDtypeStruct(shape, F32)
+    like = lambda a: jax.ShapeDtypeStruct(a.shape, a.dtype)
+    arrays = (act, grad_out, r2, dgu, mix, dh, dqkv, r1, y, dx)
+    return pl.pallas_call(
+        grads_kernel,
+        name="weight_grads",
+        in_specs=[any_spec] * 10 + [vmem_spec] * 2,
+        out_specs=[any_spec] * 6 + [vmem_spec] * 2,
+        out_shape=[out(ff, width), out(width, 32, 128), out(mix.shape[0], width), out(dqkv.shape[0], width), like(y), like(dx), out(width), out(width)],
+        scratch_shapes=[pltpu.VMEM(a.shape, a.dtype) for a in arrays] + [
+            pltpu.VMEM((4, 256, width), F32), pltpu.VMEM((2, GU_BLOCK * 40, 128), F32),
+            pltpu.SemaphoreType.DMA((10,)), pltpu.SemaphoreType.DMA((4,)), pltpu.SemaphoreType.DMA((2,)), pltpu.SemaphoreType.DMA((2,))],
+        compiler_params=pltpu.CompilerParams(vmem_limit_bytes=56 << 20),
+    )(*arrays, dg1, dg2)
 
 
 def solution(mesh):
     def per_device(x_in, positions, gain_one, gain_two, w_qkv, w_out, w_gu, w_down, grad_out):
         width, groups, chans = w_qkv.shape
         ff = w_down.shape[0]
-        cos_t, sin_t = rope_tables(positions)
         qkv_rows = w_qkv.transpose(1, 2, 0).reshape(groups * chans, width)
         gu_rows = w_gu.reshape(width, 2, ff // 128, 128).transpose(0, 2, 1, 3).reshape(width * 2 * (ff // 128), 128)
         y, dx, dg1, dg2, r1, dqkv, mix, dh, r2, dgu, act = run_layer(
-            x_in, cos_t, sin_t, gain_one.reshape(1, width), gain_two.reshape(1, width), qkv_rows, w_out, gu_rows, w_down, grad_out)
-        d_down = product_call(act, grad_out, 256, True)
-        d_gu = gate_up_grad(r2, dgu)
-        d_out = product_call(mix, dh, 256, False)
-        d_qkv = product_call(dqkv, r1, 256, False).reshape(groups, chans, width).transpose(2, 0, 1)
-        return y, dx, dg1.reshape(width), dg2.reshape(width), d_qkv, d_out, d_gu, d_down
+            x_in, positions, gain_one, gain_two, qkv_rows, w_out, gu_rows, w_down, grad_out)
+        d_down, d_gu, d_out, d_qkv, y, dx, dg1, dg2 = weight_grads(act, grad_out, r2, dgu, mix, dh, dqkv, r1, y, dx, dg1, dg2)
+        d_gu = d_gu.reshape(width, ff // 128, 2, 128).transpose(0, 2, 1, 3).reshape(width, 2, ff)
+        d_qkv = d_qkv.reshape(groups, chans, width).transpose(2, 0, 1)
+        return y, dx, dg1, dg2, d_qkv, d_out, d_gu, d_down
 
     act_spec = P('dp', 'embed')
     in_specs = (act_spec, P('dp'), P('embed'), P('embed'), P('embed', 'heads', None), P('heads', 'embed'), P('embed', None, 'heads'), P('heads', 'embed'), act_spec)

time: 208 us -> 182 us (0.88)
  Pallas kernels: 197 us -> 181 us
  local copies, waits for them, and re-layouts: 7.08 us -> 0 us
  other arithmetic: 2.83 us -> 0 us
    pallas_call x4 -> x1, Pallas kernels: 41.1 us -> 25.4 us  [weight_grads(): pl.pallas_call(grads_kernel, name='weight_grads', in_specs=[any_spec] * 1...]
    unnamed x14 -> x0, local copies, waits for them, and re-layouts: 4.49 us -> none
    reshape x2 -> x0, local copies, waits for them, and re-layouts: 2.59 us -> none  [the longest x1 1.29 us: per_device(): gain_one.reshape(1, width)]
where the time goes in v2:
time: 182 us
  Pallas kernels  181 us (99%)
    pallas_call x1, Pallas kernels, run_layer(): pl.pallas_call(layer_kernel, name='layer', out_shape=(act(width), act(wid...  156 us
    pallas_call x1, Pallas kernels, weight_grads(): pl.pallas_call(grads_kernel, name='weight_grads', in_specs=[any_spec] * 1...  25.4 us

profile of v2, /device:TPU:0, one launch (start us, length us, event | category | flops | bytes accessed | tf_op | source)
XLA Modules:
  0.0 181.7 jit_solution(10331798604282977580)
XLA Ops:
  0.6 155.6 %layer.1 = (bf16[256,1536]{1,0:T(8,128)(2,1)}, bf16[256,1536]{1,0:T(8,128)(2,1)}, f32[1,1536]{1,0:T(1,128)}, f32[1,1536]{1,0:T(1,128)}, bf16[256,1536]{1,0:T(8,1...) custom-call(bf16[256,1536]{1,0:T(8,128)(2,1)} %x_hbm.1, ...), custom_call_target="tpu_custom_call" | custom-call | tf_op jit(solution)/shard_map/layer/pallas_call | solution.py:504
  156.2 25.4 %weight_grads.1 = (f32[2048,1536]{1,0:T(8,128)}, f32[1536,32,128]{2,1,0:T(8,128)}, f32[768,1536]{1,0:T(8,128)}, f32[2304,1536]{1,0:T(8,128)}, bf16[256,1536]{1,0...) custom-call(bf16[256,2048]{1,0:T(8,128)(2,1)} %get-tuple-element.27.act_hbm, ...), custom_call_target="tpu_custom_call" | custom-call | tf_op jit(solution)/shard_map/weight_grads/pallas_call | solution.py:614

commit v3 on v2

--- a/solution.py
+++ b/solution.py
@@ -18,6 +18,8 @@
 F32 = jnp.float32
 
 AR_OUT, AR_R2, AR_Y, AR_R1 = range(4)
+SLOT = (0, 1, 2, 0)
+GU_PIECES = 4
 
 
 def dot_nn(lhs, rhs):
@@ -43,12 +45,13 @@
 def layer_kernel(x_hbm, dy_hbm, g1_in, g2_in, pos_in, wqkv_hbm, wout_hbm, wgu_hbm, wdown_hbm,
                  y_hbm, dx_hbm, dg1_ref, dg2_ref, r1_hbm, dqkv_hbm, mix_hbm, dh_hbm, r2_hbm, dgu_hbm, act_hbm,
                  x_ref, dy_ref, wqkv_ref, wout_ref, wg_ref, wu_ref, wdown_ref, raw_ref,
-                 g1_ref, g2_ref, cos_ref, sin_ref, r1_ref, r2_ref, h_ref, dh_ref, act_ref, dgu_ref, rot_ref, prob_ref, mix_ref, dqkv_ref, dx_ref,
+                 g1_ref, g2_ref, cos_ref, sin_ref, r1_ref, r2_ref, h_ref, dh_ref, act_ref, dgu_ref, rot_ref, late_ref, early_ref, mix_ref, dqkv_ref, dx_ref,
+                 kv_part, cot_ref, dots_ref,
                  inv1_ref, inv2_ref,
                  ga_send, ga_recv, qkv_send, qkv_recv, gu_send, gu_recv, gm_send, gm_recv, stat_send, stat_recv,
                  part_ref, sib_ref, half_ref, far_ref, full_ref,
                  load_sem, raw_sem, store_sem,
-                 st_s, st_r, ga_s, ga_r, qk_s, qk_r, gu_s, gu_r, gm_s, gm_r, p1_s, p1_r, p2_s, p2_r, p3_s, p3_r):
+                 st_s, st_r, ga_s, ga_r, qk_s, qk_r, gu_s, gu_r, gm_s, gm_r, p1_s, p1_r, p2_s, p2_r, p3_s, p3_r, dots_s, dots_r):
     tokens, width = x_ref.shape
     full_width = 2 * width
     ff = wdown_ref.shape[0]
@@ -63,7 +66,8 @@
     partner = {"embed": 1 - emb}
 
     barrier = pltpu.get_barrier_semaphore()
-    for peer in (sibling, across, partner):
+    others = [{"embed": lax.rem(emb + n // 4, 2), "heads": lax.rem(hid + n, 4)} for n in range(1, 8)]
+    for peer in others:
         pl.semaphore_signal(barrier, inc=1, device_id=peer, device_id_type=MESH)
 
     def load(src, dst, sem):
@@ -102,12 +106,12 @@
         r = step(j, GROUP)
         return send(qkv_send.at[r], qkv_recv.at[r], qk_s.at[j], qk_r.at[j], partner)
 
-    gu_cols = ff // 2
-
-    def gu_copy(c, p):
-        col = (p % 2) * ff + (p // 2) * gu_cols
-        at = (pl.ds(c * rows, rows), pl.ds(col, gu_cols))
-        return send(gu_send.at[at], gu_recv.at[at], gu_s.at[4 * c + p], gu_r.at[4 * c + p], partner)
+    gu_cols = ff // GU_PIECES
+
+    def gu_copy(c, q, k):
+        at = (pl.ds(c * rows, rows), pl.ds(pl.multiple_of(k * ff + q * gu_cols, gu_cols), gu_cols))
+        n = (c * GU_PIECES + q) * 2 + k
+        return send(gu_send.at[at], gu_recv.at[at], gu_s.at[n], gu_r.at[n], partner)
 
     def gm_copy(c):
         at = (slice(None), pl.ds(c * rows, rows))
@@ -119,28 +123,28 @@
     def p1_copy(i, c):
         r = pl.ds(c * rows, rows)
         k = i * CHUNKS + c
-        return send(part_ref.at[i, r, other], sib_ref.at[i, r], p1_s.at[k], p1_r.at[k], sibling)
+        return send(part_ref.at[SLOT[i], r, other], sib_ref.at[SLOT[i], r], p1_s.at[k], p1_r.at[k], sibling)
 
     def p2_copy(i, c):
         r = pl.ds(c * rows, rows)
         k = i * CHUNKS + c
-        return send(half_ref.at[i, r], far_ref.at[i, r], p2_s.at[k], p2_r.at[k], across)
+        return send(half_ref.at[SLOT[i], r], far_ref.at[SLOT[i], r], p2_s.at[k], p2_r.at[k], across)
 
     def p3_copy(i, c):
         r = pl.ds(c * rows, rows)
         k = i * CHUNKS + c
-        return send(full_ref.at[i, r, own], full_ref.at[i, r, own], p3_s.at[k], p3_r.at[k], sibling)
+        return send(full_ref.at[SLOT[i], r, own], full_ref.at[SLOT[i], r, own], p3_s.at[k], p3_r.at[k], sibling)
 
     def stage2(i, c):
         r = pl.ds(c * rows, rows)
         p1_copy(i, c).wait_recv()
-        half_ref[i, r, :] = add_bf(part_ref[i, r, own], sib_ref[i, r, :])
+        half_ref[SLOT[i], r, :] = add_bf(part_ref[SLOT[i], r, own], sib_ref[SLOT[i], r, :])
         p2_copy(i, c).start()
 
     def stage3(i, c):
         r = pl.ds(c * rows, rows)
         p2_copy(i, c).wait_recv()
-        full_ref[i, r, own] = add_bf(half_ref[i, r, :], far_ref[i, r, :])
+        full_ref[SLOT[i], r, own] = add_bf(half_ref[SLOT[i], r, :], far_ref[SLOT[i], r, :])
         p3_copy(i, c).start()
 
     def stage4(i, c):
@@ -155,13 +159,34 @@
         stat_copy(k).wait_recv()
         total = stat_send[k, 0:1, 0:n] + stat_recv[k, 0:1, 0:n]
         return jnp.broadcast_to(total, (128, n)).T[:, 0:1]
+
+    me = emb * 4 + hid
+
+    def dots_copy(k, n):
+        at = dots_ref.at[k, me]
+        return send(at, at, dots_s.at[7 * k + n], dots_r.at[8 * k + me], others[n])
+
+    def dots_put(k, col):
+        dots_ref[k, me] = jnp.broadcast_to(col, (rows, 128)).T[0:8, :]
+        for n in range(7):
+            dots_copy(k, n).start()
+
+    def dots_get(k):
+        for n in range(7):
+            src = lax.rem(emb + (n + 1) // 4, 2) * 4 + lax.rem(hid + n + 1, 4)
+            at = dots_ref.at[k, src]
+            send(at, at, dots_s.at[7 * k + n], dots_r.at[8 * k + src], others[n]).wait_recv()
+        total = dots_ref[k, 0, 0:1, :]
+        for n in range(1, 8):
+            total = total + dots_ref[k, n, 0:1, :]
+        return jnp.broadcast_to(total, (128, rows)).T[:, 0:1]
 
     g1_ref[...] = g1_in[...].reshape(1, width)
     g2_ref[...] = g2_in[...].reshape(1, width)
     loads[0].wait()
     x32 = x_ref[...].astype(F32)
     sq1 = jnp.sum(x32 * x32, axis=-1, keepdims=True)
-    pl.semaphore_wait(barrier, 3)
+    pl.semaphore_wait(barrier, 7)
     stat_put(0, sq1, tokens)
     for copy in loads[3:]:
         copy.start()
@@ -263,7 +288,8 @@
         scores = jnp.where(causal, dot_tn(k, q) * scale, -1e30)
         weight = jnp.exp(scores - jnp.max(scores, axis=0, keepdims=True))
         prob = weight / jnp.sum(weight, axis=0, keepdims=True)
-        prob_ref[j] = prob
+        late_ref[j] = prob[:, rows:]
+        early_ref[j] = prob[0:rows, 0:rows]
         mix_ref[pl.ds(pl.multiple_of(j * HEAD, 32), HEAD), :] = dot_nn(v, prob.astype(BF)).astype(BF)
         return carry
 
@@ -271,18 +297,19 @@
     stores.append(store(mix_ref, mix_hbm, 1))
 
     loads[4].wait()
-    for c in range(CHUNKS):
-        r = pl.ds(c * rows, rows)
-        part_ref[AR_OUT, r, :] = dot_tn(mix_ref[:, c * rows:(c + 1) * rows], wout_ref[...]).astype(BF)
+    order = tuple(reversed(range(CHUNKS)))
+    for c in order:
+        r = pl.ds(c * rows, rows)
+        part_ref[SLOT[AR_OUT], r, :] = dot_tn(mix_ref[:, c * rows:(c + 1) * rows], wout_ref[...]).astype(BF)
         p1_copy(AR_OUT, c).start()
-    for c in range(CHUNKS):
+    for c in order:
         stage2(AR_OUT, c)
-    for c in range(CHUNKS):
+    for c in order:
         stage3(AR_OUT, c)
-    for c in range(CHUNKS):
+    for c in order:
         r = pl.ds(c * rows, rows)
         stage4(AR_OUT, c)
-        h = add_bf(x_ref[r, :], full_ref[AR_OUT, r, :])
+        h = add_bf(x_ref[r, :], full_ref[SLOT[AR_OUT], r, :])
         h_ref[r, :] = h
         h32 = h.astype(F32)
         stat_put(1 + c, jnp.sum(h32 * h32, axis=-1, keepdims=True), rows)
@@ -290,37 +317,39 @@
         ga_copy(k).start()
 
     tile = 512
-    for c in range(CHUNKS):
+    for c in order:
         r = pl.ds(c * rows, rows)
         inv2 = lax.rsqrt(stat_get(1 + c, rows) / full_width + EPSILON)
         inv2_ref[r, :] = inv2
-        r2 = (h_ref[r, :].astype(F32) * inv2 * g2_ref[...]).astype(BF)
-        r2_ref[r, :] = r2
-        for p in range(4):
-            w_ref = (wg_ref, wu_ref)[p % 2]
-
-            def gu_body(n, carry, c=c, p=p, w_ref=w_ref):
-                src = pl.ds(pl.multiple_of((p // 2) * gu_cols + n * tile, tile), tile)
-                dst = pl.ds(pl.multiple_of((p % 2) * ff + (p // 2) * gu_cols + n * tile, tile), tile)
-                gu_send[pl.ds(c * rows, rows), dst] = dot_nn(r2_ref[pl.ds(c * rows, rows), :], w_ref[:, src]).astype(BF)
-                return carry
-
-            lax.fori_loop(0, gu_cols // tile, gu_body, 0)
-            gu_copy(c, p).start()
+        r2_ref[r, :] = (h_ref[r, :].astype(F32) * inv2 * g2_ref[...]).astype(BF)
+
+        def gu_body(q, carry, c=c, r=r):
+            for k, w_ref in ((0, wg_ref), (1, wu_ref)):
+                dst = pl.ds(pl.multiple_of(k * ff + q * gu_cols, gu_cols), gu_cols)
+                gu_send[r, dst] = dot_nn(r2_ref[r, :], w_ref[:, step(q, gu_cols)]).astype(BF)
+                gu_copy(c, q, k).start()
+            return carry
+
+        lax.fori_loop(0, GU_PIECES, gu_body, 0)
     stores.append(store(r2_ref, r2_hbm, 2))
 
     for k in range(8):
         ga_copy(k).wait_recv()
+    for c in order:
+        p1_copy(AR_OUT, c).wait_send()
+        p2_copy(AR_OUT, c).wait_send()
+        p3_copy(AR_OUT, c).wait_send()
 
     def mlp_chunk(c):
         r = pl.ds(c * rows, rows)
-        for hf in range(2):
-            gu_copy(c, 2 * hf).wait_recv()
-            gu_copy(c, 2 * hf + 1).wait_recv()
-
-            def act_body(n, carry, hf=hf):
-                cg = pl.ds(pl.multiple_of(hf * gu_cols + n * 256, 256), 256)
-                cu = pl.ds(pl.multiple_of(ff + hf * gu_cols + n * 256, 256), 256)
+        cot_ref[...] = jnp.zeros_like(cot_ref)
+
+        def piece(q, carry):
+            gu_copy(c, q, 0).wait_recv()
+            gu_copy(c, q, 1).wait_recv()
+            for n in range(gu_cols // 256):
+                cg = pl.ds(pl.multiple_of(q * gu_cols + n * 256, 256), 256)
+                cu = pl.ds(pl.multiple_of(ff + q * gu_cols + n * 256, 256), 256)
                 gate = add_bf(gu_send[r, cg], gu_recv[r, cg]).astype(F32)
                 up = add_bf(gu_send[r, cu], gu_recv[r, cu]).astype(F32)
                 ga = add_bf(ga_send[r, cg], ga_recv[r, cg]).astype(F32)
@@ -329,137 +358,156 @@
                 act_ref[r, cg] = (silu * up).astype(BF)
                 dgu_ref[r, cg] = (ga * up * (sig * (1.0 + gate * (1.0 - sig)))).astype(BF)
                 dgu_ref[r, cu] = (ga * silu).astype(BF)
-                return carry
-
-            lax.fori_loop(0, gu_cols // 256, act_body, 0)
-
-        def r2_body(n, carry):
-            w = step(n, tile)
-            part_ref[AR_R2, r, w] = (dot_nt(dgu_ref[r, 0:ff], wg_ref[w, :]) + dot_nt(dgu_ref[r, ff:2 * ff], wu_ref[w, :])).astype(BF)
+            at_g = step(q, gu_cols)
+            at_u = pl.ds(pl.multiple_of(ff + q * gu_cols, gu_cols), gu_cols)
+            for n in range(width // tile):
+                w = slice(n * tile, (n + 1) * tile)
+                cot_ref[:, w] += dot_nt(dgu_ref[r, at_g], wg_ref[w, at_g]) + dot_nt(dgu_ref[r, at_u], wu_ref[w, at_g])
             return carry
 
-        lax.fori_loop(0, width // tile, r2_body, 0)
+        lax.fori_loop(0, GU_PIECES, piece, 0)
+        part_ref[SLOT[AR_R2], r, :] = cot_ref[...].astype(BF)
         p1_copy(AR_R2, c).start()
+        unit = h_ref[r, :].astype(F32) * inv2_ref[r, :]
+        dots_put(c, jnp.sum(cot_ref[...] * g2_ref[...] * unit, axis=-1, keepdims=True))
 
     def down_chunk(c):
         r = pl.ds(c * rows, rows)
 
         def down_body(n, carry):
             w = step(n, tile)
-            part_ref[AR_Y, r, w] = dot_nn(act_ref[r, :], wdown_ref[:, w]).astype(BF)
+            part_ref[SLOT[AR_Y], r, w] = dot_nn(act_ref[r, :], wdown_ref[:, w]).astype(BF)
             return carry
 
         lax.fori_loop(0, width // tile, down_body, 0)
         p1_copy(AR_Y, c).start()
 
+    dg1_ref[...] = jnp.zeros_like(dg1_ref)
     dg2_ref[...] = jnp.zeros_like(dg2_ref)
 
-    def norm2_back(c):
-        r = pl.ds(c * rows, rows)
+    def hidden_back(c):
+        r = pl.ds(c * rows, rows)
+        dots = dots_get(c)
         stage4(AR_R2, c)
-        gin = full_ref[AR_R2, r, :].astype(F32)
-        unit = h_ref[r, :].astype(F32) * inv2_ref[r, :]
-        dg2_ref[...] += jnp.sum(gin * unit, axis=0, keepdims=True)
-        stat_put(3 + c, jnp.sum(gin * g2_ref[...] * unit, axis=-1, keepdims=True), rows)
-
-    def hidden_back(c):
-        r = pl.ds(c * rows, rows)
-        dots = stat_get(3 + c, rows)
         inv2 = inv2_ref[r, :]
         unit = h_ref[r, :].astype(F32) * inv2
-        scaled = full_ref[AR_R2, r, :].astype(F32) * g2_ref[...]
-        norm = inv2 * (scaled - unit * (dots / full_width))
+        gin = full_ref[SLOT[AR_R2], r, :].astype(F32)
+        norm = inv2 * (gin * g2_ref[...] - unit * (dots / full_width))
         dh_ref[r, :] = (dy_ref[r, :].astype(F32) + norm).astype(BF)
         gm_send[:, c * rows:(c + 1) * rows] = dot_nt(wout_ref[...], dh_ref[r, :]).astype(BF)
         gm_copy(c).start()
+        dg2_ref[...] += jnp.sum(gin * unit, axis=0, keepdims=True)
 
     def y_chunk(c):
         r = pl.ds(c * rows, rows)
         stage4(AR_Y, c)
-        h_ref[r, :] = add_bf(h_ref[r, :], full_ref[AR_Y, r, :])
-
-    mlp_chunk(0)
-    down_chunk(0)
-    stage2(AR_R2, 0)
-    stage3(AR_R2, 0)
-    stage2(AR_Y, 0)
-    norm2_back(0)
-    stage3(AR_Y, 0)
-    mlp_chunk(1)
-    stores.append(store(dgu_ref, dgu_hbm, 3))
-    stores.append(store(act_ref, act_hbm, 4))
-    stage2(AR_R2, 1)
-    hidden_back(0)
-    stage3(AR_R2, 1)
-    norm2_back(1)
-    down_chunk(1)
-    hidden_back(1)
-    stores.append(store(dh_ref, dh_hbm, 5))
-    stage2(AR_Y, 1)
-    y_chunk(0)
-    stage3(AR_Y, 1)
-    y_chunk(1)
-    stores.append(store(h_ref, y_hbm, 6))
-
-    for c in range(CHUNKS):
-        gm_copy(c).wait_recv()
-
-    def back_body(j, carry):
+        h_ref[r, :] = add_bf(h_ref[r, :], full_ref[SLOT[AR_Y], r, :])
+
+    def scores_back(v, da, prob):
+        dp = dot_tn(v, da).astype(BF).astype(F32)
+        weighted = prob * dp
+        return ((weighted - prob * jnp.sum(weighted, axis=0, keepdims=True)) * scale).astype(BF)
+
+    def late_body(j, carry):
         base = pl.multiple_of(j * GROUP, 32)
         r_q, r_k, r_v = (pl.ds(base + n * HEAD, HEAD) for n in range(3))
         r_a = pl.ds(pl.multiple_of(j * HEAD, 32), HEAD)
-        cos_t, sin_t = cos_ref[...], sin_ref[...]
-        da = add_bf(gm_send[r_a, :], gm_recv[r_a, :])
-        q, k, v = rot_ref[r_q, :], rot_ref[r_k, :], rot_ref[r_v, :]
-        prob = prob_ref[j]
-        dp = dot_tn(v, da).astype(BF).astype(F32)
-        dqkv_ref[r_v, :] = dot_nt(da, prob.astype(BF)).astype(BF)
-        weighted = prob * dp
-        ds = ((weighted - prob * jnp.sum(weighted, axis=0, keepdims=True)) * scale).astype(BF)
-        dqkv_ref[r_q, :] = unrope(dot_nn(k, ds).astype(BF), cos_t, sin_t)
-        dqkv_ref[r_k, :] = unrope(dot_nt(q, ds).astype(BF), cos_t, sin_t)
+        cos_t, sin_t = cos_ref[:, rows:], sin_ref[:, rows:]
+        da = add_bf(gm_send[r_a, rows:], gm_recv[r_a, rows:])
+        prob = late_ref[j]
+        k = rot_ref[r_k, :]
+        ds = scores_back(rot_ref[r_v, :], da, prob)
+        dv = dot_nt(da, prob.astype(BF))
+        dk = dot_nt(rot_ref[r_q, rows:], ds)
+        dqkv_ref[r_q, rows:] = unrope(dot_nn(k, ds).astype(BF), cos_t, sin_t)
+        dqkv_ref[r_k, rows:] = unrope(dk[:, rows:].astype(BF), cos_t, sin_t)
+        dqkv_ref[r_v, rows:] = dv[:, rows:].astype(BF)
+        kv_part[0, r_a, :] = dk[:, 0:rows]
+        kv_part[1, r_a, :] = dv[:, 0:rows]
         return carry
 
-    lax.fori_loop(0, heads, back_body, 0)
-    stores.append(store(dqkv_ref, dqkv_hbm, 7))
-
-    for c in range(CHUNKS):
-        r = pl.ds(c * rows, rows)
-        part_ref[AR_R1, r, :] = dot_tn(dqkv_ref[:, c * rows:(c + 1) * rows], wqkv_ref[...]).astype(BF)
+    def early_body(j, carry):
+        base = pl.multiple_of(j * GROUP, 32)
+        r_q, r_k, r_v = (pl.ds(base + n * HEAD, HEAD) for n in range(3))
+        r_a = pl.ds(pl.multiple_of(j * HEAD, 32), HEAD)
+        cos_t, sin_t = cos_ref[:, 0:rows], sin_ref[:, 0:rows]
+        da = add_bf(gm_send[r_a, 0:rows], gm_recv[r_a, 0:rows])
+        prob = early_ref[j]
+        ds = scores_back(rot_ref[r_v, 0:rows], da, prob)
+        dv = kv_part[1, r_a, :] + dot_nt(da, prob.astype(BF))
+        dk = kv_part[0, r_a, :] + dot_nt(rot_ref[r_q, 0:rows], ds)
+        dqkv_ref[r_q, 0:rows] = unrope(dot_nn(rot_ref[r_k, 0:rows], ds).astype(BF), cos_t, sin_t)
+        dqkv_ref[r_k, 0:rows] = unrope(dk.astype(BF), cos_t, sin_t)
+        dqkv_ref[r_v, 0:rows] = dv.astype(BF)
+        return carry
+
+    def attn_back(c):
+        gm_copy(c).wait_recv()
+        lax.fori_loop(0, heads, late_body if c else early_body, 0)
+        r = pl.ds(c * rows, rows)
+        cot = dot_tn(dqkv_ref[:, c * rows:(c + 1) * rows], wqkv_ref[...])
+        part_ref[SLOT[AR_R1], r, :] = cot.astype(BF)
         p1_copy(AR_R1, c).start()
-    for c in range(CHUNKS):
-        stage2(AR_R1, c)
-    for c in range(CHUNKS):
-        stage3(AR_R1, c)
-    dg1_ref[...] = jnp.zeros_like(dg1_ref)
-    for c in range(CHUNKS):
-        r = pl.ds(c * rows, rows)
+        unit = x_ref[r, :].astype(F32) * inv1_ref[r, :]
+        dots_put(CHUNKS + c, jnp.sum(cot * g1_ref[...] * unit, axis=-1, keepdims=True))
+
+    def input_back(c):
+        r = pl.ds(c * rows, rows)
+        dots = dots_get(CHUNKS + c)
         stage4(AR_R1, c)
-        gin = full_ref[AR_R1, r, :].astype(F32)
-        unit = x_ref[r, :].astype(F32) * inv1_ref[r, :]
-        dg1_ref[...] += jnp.sum(gin * unit, axis=0, keepdims=True)
-        stat_put(5 + c, jnp.sum(gin * g1_ref[...] * unit, axis=-1, keepdims=True), rows)
-    for c in range(CHUNKS):
-        r = pl.ds(c * rows, rows)
-        dots = stat_get(5 + c, rows)
         inv1 = inv1_ref[r, :]
         unit = x_ref[r, :].astype(F32) * inv1
-        scaled = full_ref[AR_R1, r, :].astype(F32) * g1_ref[...]
-        norm = inv1 * (scaled - unit * (dots / full_width))
+        gin = full_ref[SLOT[AR_R1], r, :].astype(F32)
+        norm = inv1 * (gin * g1_ref[...] - unit * (dots / full_width))
         dx_ref[r, :] = (dh_ref[r, :].astype(F32) + norm).astype(BF)
-    stores.append(store(dx_ref, dx_hbm, 8))
-
-    for k in range(7):
+        stores.append(store(dx_ref.at[r], dx_hbm.at[r], 8 + c))
+        dg1_ref[...] += jnp.sum(gin * unit, axis=0, keepdims=True)
+
+    mlp_chunk(1)
+    stage2(AR_R2, 1)
+    down_chunk(1)
+    stage3(AR_R2, 1)
+    stage2(AR_Y, 1)
+    hidden_back(1)
+    stage3(AR_Y, 1)
+    mlp_chunk(0)
+    stage2(AR_R2, 0)
+    stores.append(store(dgu_ref, dgu_hbm, 3))
+    stores.append(store(act_ref, act_hbm, 4))
+    attn_back(1)
+    stage3(AR_R2, 0)
+    stage2(AR_R1, 1)
+    hidden_back(0)
+    stores.append(store(dh_ref, dh_hbm, 5))
+    down_chunk(0)
+    stage3(AR_R1, 1)
+    stage2(AR_Y, 0)
+    y_chunk(1)
+    attn_back(0)
+    stores.append(store(dqkv_ref, dqkv_hbm, 7))
+    stage2(AR_R1, 0)
+    stage3(AR_Y, 0)
+    input_back(1)
+    y_chunk(0)
+    stores.append(store(h_ref, y_hbm, 6))
+    stage3(AR_R1, 0)
+    input_back(0)
+
+    for k in range(3):
         stat_copy(k).wait_send()
+    for k in range(2 * CHUNKS):
+        for n in range(7):
+            dots_copy(k, n).wait_send()
     for k in range(8):
         ga_copy(k).wait_send()
     for j in range(heads):
         qkv_copy(j).wait_send()
     for c in range(CHUNKS):
-        for p in range(4):
-            gu_copy(c, p).wait_send()
+        for q in range(GU_PIECES):
+            for k in range(2):
+                gu_copy(c, q, k).wait_send()
         gm_copy(c).wait_send()
-        for i in range(4):
+        for i in range(1, 4):
             p1_copy(i, c).wait_send()
             p2_copy(i, c).wait_send()
             p3_copy(i, c).wait_send()
@@ -486,20 +534,22 @@
         pltpu.VMEM((1, width), F32), pltpu.VMEM((1, width), F32), pltpu.VMEM((HALF, tokens), F32), pltpu.VMEM((HALF, tokens), F32),
         pltpu.VMEM((tokens, width), BF), pltpu.VMEM((tokens, width), BF), pltpu.VMEM((tokens, width), BF), pltpu.VMEM((tokens, width), BF),
         pltpu.VMEM((tokens, ff), BF), pltpu.VMEM((tokens, 2 * ff), BF),
-        pltpu.VMEM((chans, tokens), BF), pltpu.VMEM((heads, tokens, tokens), F32), pltpu.VMEM((mix, tokens), BF), pltpu.VMEM((chans, tokens), BF),
+        pltpu.VMEM((chans, tokens), BF), pltpu.VMEM((heads, tokens, rows), F32), pltpu.VMEM((heads, rows, rows), F32), pltpu.VMEM((mix, tokens), BF), pltpu.VMEM((chans, tokens), BF),
         pltpu.VMEM((tokens, width), BF),
+        pltpu.VMEM((2, mix, rows), F32), pltpu.VMEM((rows, width), F32), pltpu.VMEM((2 * CHUNKS, 8, 8, rows), F32),
         pltpu.VMEM((tokens, 1), F32), pltpu.VMEM((tokens, 1), F32),
         pltpu.VMEM((tokens, ff), BF), pltpu.VMEM((tokens, ff), BF),
         pltpu.VMEM((chans, tokens), BF), pltpu.VMEM((chans, tokens), BF),
         pltpu.VMEM((tokens, 2 * ff), BF), pltpu.VMEM((tokens, 2 * ff), BF),
         pltpu.VMEM((mix, tokens), BF), pltpu.VMEM((mix, tokens), BF),
-        pltpu.VMEM((7, 8, tokens), F32), pltpu.VMEM((7, 8, tokens), F32),
-        pltpu.VMEM((4, tokens, width), BF), pltpu.VMEM((4, tokens, width // 2), BF), pltpu.VMEM((4, tokens, width // 2), BF),
-        pltpu.VMEM((4, tokens, width // 2), BF), pltpu.VMEM((4, tokens, width), BF),
-        pltpu.SemaphoreType.DMA((5,)), pltpu.SemaphoreType.DMA((2,)), pltpu.SemaphoreType.DMA((9,)),
+        pltpu.VMEM((3, 8, tokens), F32), pltpu.VMEM((3, 8, tokens), F32),
+        pltpu.VMEM((3, tokens, width), BF), pltpu.VMEM((3, tokens, width // 2), BF), pltpu.VMEM((3, tokens, width // 2), BF),
+        pltpu.VMEM((3, tokens, width // 2), BF), pltpu.VMEM((3, tokens, width), BF),
+        pltpu.SemaphoreType.DMA((5,)), pltpu.SemaphoreType.DMA((2,)), pltpu.SemaphoreType.DMA((8 + CHUNKS,)),
     ]
-    for n in (7, 8, heads, 4 * CHUNKS, CHUNKS, 4 * CHUNKS, 4 * CHUNKS, 4 * CHUNKS):
+    for n in (3, 8, heads, 2 * GU_PIECES * CHUNKS, CHUNKS, 4 * CHUNKS, 4 * CHUNKS, 4 * CHUNKS):
         scratch += [pltpu.SemaphoreType.DMA((n,)), pltpu.SemaphoreType.DMA((n,))]
+    scratch += [pltpu.SemaphoreType.DMA((7 * 2 * CHUNKS,)), pltpu.SemaphoreType.DMA((8 * 2 * CHUNKS,))]
     vec = jax.ShapeDtypeStruct((1, width), F32)
     return pl.pallas_call(
         layer_kernel,

time: 182 us -> 175 us (0.962)
  Pallas kernels: 181 us -> 174 us
    pallas_call x1, Pallas kernels: 156 us -> 148 us  [run_layer(): pl.pallas_call(layer_kernel, name='layer', out_shape=(act(width), act(wid...]
where the time goes in v3:
time: 175 us; the launch traced here: 174 us
  Pallas kernels  174 us (99%)
    pallas_call x1, Pallas kernels, run_layer(): pl.pallas_call(layer_kernel, name='layer', out_shape=(act(width), act(wid...  148 us
    pallas_call x1, Pallas kernels, weight_grads(): pl.pallas_call(grads_kernel, name='weight_grads', in_specs=[any_spec] * 1...  25.4 us

profile of v3, /device:TPU:0, one launch (start us, length us, event | category | flops | bytes accessed | tf_op | source)
XLA Modules:
  0.0 174.4 jit_solution(5024766118358191359)
XLA Ops:
  0.6 148.3 %layer.1 = (bf16[256,1536]{1,0:T(8,128)(2,1)}, bf16[256,1536]{1,0:T(8,128)(2,1)}, f32[1,1536]{1,0:T(1,128)}, f32[1,1536]{1,0:T(1,128)}, bf16[256,1536]{1,0:T(8,1...) custom-call(bf16[256,1536]{1,0:T(8,128)(2,1)} %x_hbm.1, ...), custom_call_target="tpu_custom_call" | custom-call | tf_op jit(solution)/shard_map/layer/pallas_call | solution.py:554
  148.9 25.4 %weight_grads.1 = (f32[2048,1536]{1,0:T(8,128)}, f32[1536,32,128]{2,1,0:T(8,128)}, f32[768,1536]{1,0:T(8,128)}, f32[2304,1536]{1,0:T(8,128)}, bf16[256,1536]{1,0...) custom-call(bf16[256,2048]{1,0:T(8,128)(2,1)} %get-tuple-element.27.act_hbm, ...), custom_call_target="tpu_custom_call" | custom-call | tf_op jit(solution)/shard_map/weight_grads/pallas_call | solution.py:664

commit v4 on v3

--- a/solution.py
+++ b/solution.py
@@ -113,9 +113,11 @@
         n = (c * GU_PIECES + q) * 2 + k
         return send(gu_send.at[at], gu_recv.at[at], gu_s.at[n], gu_r.at[n], partner)
 
-    def gm_copy(c):
-        at = (slice(None), pl.ds(c * rows, rows))
-        return send(gm_send.at[at], gm_recv.at[at], gm_s.at[c], gm_r.at[c], partner)
+    gm_rows = gm_send.shape[0] // 2
+
+    def gm_copy(c, hf):
+        at = (pl.ds(hf * gm_rows, gm_rows), pl.ds(c * rows, rows))
+        return send(gm_send.at[at], gm_recv.at[at], gm_s.at[2 * c + hf], gm_r.at[2 * c + hf], partner)
 
     own = pl.ds(pl.multiple_of(core * half_width, half_width), half_width)
     other = pl.ds(pl.multiple_of((1 - core) * half_width, half_width), half_width)
@@ -181,38 +183,33 @@
             total = total + dots_ref[k, n, 0:1, :]
         return jnp.broadcast_to(total, (128, rows)).T[:, 0:1]
 
+    place = pos_in[...].reshape(1, tokens).astype(F32)
+    pair_i = lax.broadcasted_iota(jnp.int32, (HALF, 1), 0).astype(F32)
+    angles = jnp.exp(pair_i * (-2.0 * math.log(ROPE_BASE) / HEAD)) * place
+    cos_ref[...] = jnp.cos(angles)
+    sin_ref[...] = jnp.sin(angles)
     g1_ref[...] = g1_in[...].reshape(1, width)
     g2_ref[...] = g2_in[...].reshape(1, width)
     loads[0].wait()
     x32 = x_ref[...].astype(F32)
     sq1 = jnp.sum(x32 * x32, axis=-1, keepdims=True)
-    pl.semaphore_wait(barrier, 7)
-    stat_put(0, sq1, tokens)
     for copy in loads[3:]:
         copy.start()
     for slot in range(2):
         raw_load(slot, slot).start()
 
-    loads[1].wait()
-    loads[2].wait()
-
     def ga_body(k, carry):
         cols = step(k, ga_cols)
         ga_send[:, cols] = dot_nt(dy_ref[...], wdown_ref[cols, :]).astype(BF)
-
-        @pl.when(k == 0)
-        def _():
-            ga_copy(k).start()
         return carry
 
-    lax.fori_loop(0, 8, ga_body, 0)
-
-    place = pos_in[...].reshape(1, tokens).astype(F32)
-    pair_i = lax.broadcasted_iota(jnp.int32, (HALF, 1), 0).astype(F32)
-    angles = jnp.exp(pair_i * (-2.0 * math.log(ROPE_BASE) / HEAD)) * place
-    cos_ref[...] = jnp.cos(angles)
-    sin_ref[...] = jnp.sin(angles)
-
+    loads[1].wait()
+    loads[2].wait()
+    lax.fori_loop(0, 4, ga_body, 0)
+    pl.semaphore_wait(barrier, 7)
+    stat_put(0, sq1, tokens)
+    ga_copy(0).start()
+    lax.fori_loop(4, 8, ga_body, 0)
     inv1 = lax.rsqrt(stat_get(0, tokens) / full_width + EPSILON)
     inv1_ref[...] = inv1
     r1_ref[...] = (x_ref[...].astype(F32) * inv1 * g1_ref[...]).astype(BF)
@@ -227,8 +224,6 @@
         return carry
 
     lax.fori_loop(0, heads, qkv_body, 0)
-    for k in range(1, 5):
-        ga_copy(k).start()
 
     row_i = lax.broadcasted_iota(jnp.int32, (256, 256), 0)
     col_i = lax.broadcasted_iota(jnp.int32, (256, 256), 1)
@@ -275,6 +270,11 @@
         return jnp.concatenate([one * cos_t + two * sin_t, two * cos_t - one * sin_t], axis=0).astype(BF)
 
     def attn_body(j, carry):
+        @pl.when(j == heads - 1)
+        def _():
+            qkv_copy(j).wait_send()
+            for n in range(1, 5):
+                ga_copy(n).start()
         qkv_copy(j).wait_recv()
         base = pl.multiple_of(j * GROUP, 32)
         r_q, r_k, r_v = (pl.ds(base + n * HEAD, HEAD) for n in range(3))
@@ -302,51 +302,71 @@
         r = pl.ds(c * rows, rows)
         part_ref[SLOT[AR_OUT], r, :] = dot_tn(mix_ref[:, c * rows:(c + 1) * rows], wout_ref[...]).astype(BF)
         p1_copy(AR_OUT, c).start()
-    for c in order:
-        stage2(AR_OUT, c)
-    for c in order:
-        stage3(AR_OUT, c)
-    for c in order:
+    def gu_start(c, q):
+        for k in range(2):
+            gu_copy(c, q, k).start()
+
+    def hidden_fwd(c):
         r = pl.ds(c * rows, rows)
         stage4(AR_OUT, c)
         h = add_bf(x_ref[r, :], full_ref[SLOT[AR_OUT], r, :])
         h_ref[r, :] = h
         h32 = h.astype(F32)
         stat_put(1 + c, jnp.sum(h32 * h32, axis=-1, keepdims=True), rows)
-    for k in range(5, 8):
-        ga_copy(k).start()
-
-    tile = 512
-    for c in order:
+
+    def gate_up(c, at_once):
         r = pl.ds(c * rows, rows)
         inv2 = lax.rsqrt(stat_get(1 + c, rows) / full_width + EPSILON)
         inv2_ref[r, :] = inv2
         r2_ref[r, :] = (h_ref[r, :].astype(F32) * inv2 * g2_ref[...]).astype(BF)
 
-        def gu_body(q, carry, c=c, r=r):
+        def gu_body(q, carry):
             for k, w_ref in ((0, wg_ref), (1, wu_ref)):
                 dst = pl.ds(pl.multiple_of(k * ff + q * gu_cols, gu_cols), gu_cols)
                 gu_send[r, dst] = dot_nn(r2_ref[r, :], w_ref[:, step(q, gu_cols)]).astype(BF)
-                gu_copy(c, q, k).start()
+
+            @pl.when(q < at_once)
+            def _():
+                gu_start(c, q)
             return carry
 
         lax.fori_loop(0, GU_PIECES, gu_body, 0)
+
+    stage2(AR_OUT, 1)
+    p2_copy(AR_OUT, 1).wait_send()
+    stage2(AR_OUT, 0)
+    stage3(AR_OUT, 1)
+    hidden_fwd(1)
+    for k in range(5, 8):
+        ga_copy(k).start()
+    gate_up(1, 2)
+    stage3(AR_OUT, 0)
+    hidden_fwd(0)
+    gu_start(1, 2)
+    gu_start(1, 3)
+    gate_up(0, 0)
+    tile = 512
     stores.append(store(r2_ref, r2_hbm, 2))
 
     for k in range(8):
         ga_copy(k).wait_recv()
     for c in order:
         p1_copy(AR_OUT, c).wait_send()
-        p2_copy(AR_OUT, c).wait_send()
         p3_copy(AR_OUT, c).wait_send()
-
-    def mlp_chunk(c):
-        r = pl.ds(c * rows, rows)
-        cot_ref[...] = jnp.zeros_like(cot_ref)
+    p2_copy(AR_OUT, 0).wait_send()
+
+    def mlp_pieces(c, lo, hi, then_at=None):
+        r = pl.ds(c * rows, rows)
+        if lo == 0:
+            cot_ref[...] = jnp.zeros_like(cot_ref)
 
         def piece(q, carry):
             gu_copy(c, q, 0).wait_recv()
             gu_copy(c, q, 1).wait_recv()
+            if then_at is not None:
+                @pl.when(q == then_at)
+                def _():
+                    gu_start(0, 0)
             for n in range(gu_cols // 256):
                 cg = pl.ds(pl.multiple_of(q * gu_cols + n * 256, 256), 256)
                 cu = pl.ds(pl.multiple_of(ff + q * gu_cols + n * 256, 256), 256)
@@ -365,7 +385,10 @@
                 cot_ref[:, w] += dot_nt(dgu_ref[r, at_g], wg_ref[w, at_g]) + dot_nt(dgu_ref[r, at_u], wu_ref[w, at_g])
             return carry
 
-        lax.fori_loop(0, GU_PIECES, piece, 0)
+        lax.fori_loop(lo, hi, piece, 0)
+
+    def mlp_end(c):
+        r = pl.ds(c * rows, rows)
         part_ref[SLOT[AR_R2], r, :] = cot_ref[...].astype(BF)
         p1_copy(AR_R2, c).start()
         unit = h_ref[r, :].astype(F32) * inv2_ref[r, :]
@@ -385,7 +408,7 @@
     dg1_ref[...] = jnp.zeros_like(dg1_ref)
     dg2_ref[...] = jnp.zeros_like(dg2_ref)
 
-    def hidden_back(c):
+    def hidden_back(c, then=lambda: None):
         r = pl.ds(c * rows, rows)
         dots = dots_get(c)
         stage4(AR_R2, c)
@@ -395,7 +418,9 @@
         norm = inv2 * (gin * g2_ref[...] - unit * (dots / full_width))
         dh_ref[r, :] = (dy_ref[r, :].astype(F32) + norm).astype(BF)
         gm_send[:, c * rows:(c + 1) * rows] = dot_nt(wout_ref[...], dh_ref[r, :]).astype(BF)
-        gm_copy(c).start()
+        for hf in range(2):
+            gm_copy(c, hf).start()
+        then()
         dg2_ref[...] += jnp.sum(gin * unit, axis=0, keepdims=True)
 
     def y_chunk(c):
@@ -442,8 +467,9 @@
         return carry
 
     def attn_back(c):
-        gm_copy(c).wait_recv()
-        lax.fori_loop(0, heads, late_body if c else early_body, 0)
+        for hf in range(2):
+            gm_copy(c, hf).wait_recv()
+            lax.fori_loop(hf * heads // 2, (hf + 1) * heads // 2, late_body if c else early_body, 0)
         r = pl.ds(c * rows, rows)
         cot = dot_tn(dqkv_ref[:, c * rows:(c + 1) * rows], wqkv_ref[...])
         part_ref[SLOT[AR_R1], r, :] = cot.astype(BF)
@@ -463,31 +489,40 @@
         stores.append(store(dx_ref.at[r], dx_hbm.at[r], 8 + c))
         dg1_ref[...] += jnp.sum(gin * unit, axis=0, keepdims=True)
 
-    mlp_chunk(1)
+    def rest_of_gate_up():
+        gu_start(0, 2)
+        gu_start(0, 3)
+
+    mlp_pieces(1, 0, 4, then_at=2)
+    mlp_end(1)
+    gu_start(0, 1)
     stage2(AR_R2, 1)
     down_chunk(1)
     stage3(AR_R2, 1)
     stage2(AR_Y, 1)
-    hidden_back(1)
+    hidden_back(1, rest_of_gate_up)
+    mlp_pieces(0, 0, 2)
     stage3(AR_Y, 1)
-    mlp_chunk(0)
-    stage2(AR_R2, 0)
+    attn_back(1)
+    mlp_pieces(0, 2, 3)
+    stage2(AR_R1, 1)
+    mlp_pieces(0, 3, 4)
+    mlp_end(0)
     stores.append(store(dgu_ref, dgu_hbm, 3))
     stores.append(store(act_ref, act_hbm, 4))
-    attn_back(1)
+    stage2(AR_R2, 0)
+    down_chunk(0)
+    stage3(AR_R1, 1)
+    y_chunk(1)
     stage3(AR_R2, 0)
-    stage2(AR_R1, 1)
     hidden_back(0)
     stores.append(store(dh_ref, dh_hbm, 5))
-    down_chunk(0)
-    stage3(AR_R1, 1)
     stage2(AR_Y, 0)
-    y_chunk(1)
+    input_back(1)
     attn_back(0)
     stores.append(store(dqkv_ref, dqkv_hbm, 7))
     stage2(AR_R1, 0)
     stage3(AR_Y, 0)
-    input_back(1)
     y_chunk(0)
     stores.append(store(h_ref, y_hbm, 6))
     stage3(AR_R1, 0)
@@ -500,13 +535,14 @@
             dots_copy(k, n).wait_send()
     for k in range(8):
         ga_copy(k).wait_send()
-    for j in range(heads):
+    for j in range(heads - 1):
         qkv_copy(j).wait_send()
     for c in range(CHUNKS):
         for q in range(GU_PIECES):
             for k in range(2):
                 gu_copy(c, q, k).wait_send()
-        gm_copy(c).wait_send()
+        for hf in range(2):
+            gm_copy(c, hf).wait_send()
         for i in range(1, 4):
             p1_copy(i, c).wait_send()
             p2_copy(i, c).wait_send()
@@ -547,7 +583,7 @@
         pltpu.VMEM((3, tokens, width // 2), BF), pltpu.VMEM((3, tokens, width), BF),
         pltpu.SemaphoreType.DMA((5,)), pltpu.SemaphoreType.DMA((2,)), pltpu.SemaphoreType.DMA((8 + CHUNKS,)),
     ]
-    for n in (3, 8, heads, 2 * GU_PIECES * CHUNKS, CHUNKS, 4 * CHUNKS, 4 * CHUNKS, 4 * CHUNKS):
+    for n in (3, 8, heads, 2 * GU_PIECES * CHUNKS, 2 * CHUNKS, 4 * CHUNKS, 4 * CHUNKS, 4 * CHUNKS):
         scratch += [pltpu.SemaphoreType.DMA((n,)), pltpu.SemaphoreType.DMA((n,))]
     scratch += [pltpu.SemaphoreType.DMA((7 * 2 * CHUNKS,)), pltpu.SemaphoreType.DMA((8 * 2 * CHUNKS,))]
     vec = jax.ShapeDtypeStruct((1, width), F32)

time: 175 us -> 169 us (0.966)
  Pallas kernels: 174 us -> 167 us
    pallas_call x1, Pallas kernels: 148 us -> 142 us  [run_layer(): pl.pallas_call(layer_kernel, name='layer', out_shape=(act(width), act(wid...]
where the time goes in v4:
time: 169 us; the launch traced here: 168 us
  Pallas kernels  167 us (99%)
    pallas_call x1, Pallas kernels, run_layer(): pl.pallas_call(layer_kernel, name='layer', out_shape=(act(width), act(wid...  142 us
    pallas_call x1, Pallas kernels, weight_grads(): pl.pallas_call(grads_kernel, name='weight_grads', in_specs=[any_spec] * 1...  25.4 us

profile of v4, /device:TPU:0, one launch (start us, length us, event | category | flops | bytes accessed | tf_op | source)
XLA Modules:
  0.0 168.1 jit_solution(1198137035986734647)
XLA Ops:
  0.6 142.0 %layer.1 = (bf16[256,1536]{1,0:T(8,128)(2,1)}, bf16[256,1536]{1,0:T(8,128)(2,1)}, f32[1,1536]{1,0:T(1,128)}, f32[1,1536]{1,0:T(1,128)}, bf16[256,1536]{1,0:T(8,1...) custom-call(bf16[256,1536]{1,0:T(8,128)(2,1)} %x_hbm.1, ...), custom_call_target="tpu_custom_call" | custom-call | tf_op jit(solution)/shard_map/layer/pallas_call | solution.py:590
  142.6 25.4 %weight_grads.1 = (f32[2048,1536]{1,0:T(8,128)}, f32[1536,32,128]{2,1,0:T(8,128)}, f32[768,1536]{1,0:T(8,128)}, f32[2304,1536]{1,0:T(8,128)}, bf16[256,1536]{1,0...) custom-call(bf16[256,2048]{1,0:T(8,128)(2,1)} %get-tuple-element.27.act_hbm, ...), custom_call_target="tpu_custom_call" | custom-call | tf_op jit(solution)/shard_map/weight_grads/pallas_call | solution.py:700

commit v5 on v4

--- a/solution.py
+++ b/solution.py
@@ -20,6 +20,7 @@
 AR_OUT, AR_R2, AR_Y, AR_R1 = range(4)
 SLOT = (0, 1, 2, 0)
 GU_PIECES = 4
+EARLY, LATE = 0, 1
 
 
 def dot_nn(lhs, rhs):
@@ -51,7 +52,7 @@
                  ga_send, ga_recv, qkv_send, qkv_recv, gu_send, gu_recv, gm_send, gm_recv, stat_send, stat_recv,
                  part_ref, sib_ref, half_ref, far_ref, full_ref,
                  load_sem, raw_sem, store_sem,
-                 st_s, st_r, ga_s, ga_r, qk_s, qk_r, gu_s, gu_r, gm_s, gm_r, p1_s, p1_r, p2_s, p2_r, p3_s, p3_r, dots_s, dots_r):
+                 st_s, st_r, ga_s, ga_r, qk_s, qk_r, gu_s, gu_r, gm_s, gm_r, p1_s, p1_r, p2_s, p2_r, p3_s, p3_r, dots_s, dots_r, mx_s, mx_r, rt_s, rt_r):
     tokens, width = x_ref.shape
     full_width = 2 * width
     ff = wdown_ref.shape[0]
@@ -106,6 +107,25 @@
         r = step(j, GROUP)
         return send(qkv_send.at[r], qkv_recv.at[r], qk_s.at[j], qk_r.at[j], partner)
 
+    half_heads = heads // 2
+
+    def mine(i):
+        return emb * half_heads + i
+
+    def theirs(i):
+        return (1 - emb) * half_heads + i
+
+    def mix_rows(j):
+        return pl.ds(pl.multiple_of(j * HEAD, 32), HEAD)
+
+    def mix_copy(j):
+        at = mix_ref.at[mix_rows(j)]
+        return send(at, at, mx_s.at[j], mx_r.at[j], partner)
+
+    def rot_copy(j):
+        at = rot_ref.at[step(j, GROUP)]
+        return send(at, at, rt_s.at[j], rt_r.at[j], partner)
+
     gu_cols = ff // GU_PIECES
 
     def gu_copy(c, q, k):
@@ -116,7 +136,7 @@
     gm_rows = gm_send.shape[0] // 2
 
     def gm_copy(c, hf):
-        at = (pl.ds(hf * gm_rows, gm_rows), pl.ds(c * rows, rows))
+        at = (step(hf, gm_rows), pl.ds(c * rows, rows))
         return send(gm_send.at[at], gm_recv.at[at], gm_s.at[2 * c + hf], gm_r.at[2 * c + hf], partner)
 
     own = pl.ds(pl.multiple_of(core * half_width, half_width), half_width)
@@ -217,13 +237,21 @@
 
     loads[3].wait()
 
-    def qkv_body(j, carry):
+    def qkv_product(j):
         r = step(j, GROUP)
         qkv_send[r, :] = dot_nt(wqkv_ref[r, :], r1_ref[...]).astype(BF)
-        qkv_copy(j).start()
-        return carry
-
-    lax.fori_loop(0, heads, qkv_body, 0)
+
+    def qkv_theirs(i, carry):
+        qkv_product(theirs(i))
+        qkv_copy(theirs(i)).start()
+        return carry
+
+    def qkv_mine(i, carry):
+        qkv_product(mine(i))
+        return carry
+
+    lax.fori_loop(0, half_heads, qkv_theirs, 0)
+    lax.fori_loop(0, half_heads, qkv_mine, 0)
 
     row_i = lax.broadcasted_iota(jnp.int32, (256, 256), 0)
     col_i = lax.broadcasted_iota(jnp.int32, (256, 256), 1)
@@ -254,7 +282,8 @@
             raw_load(i + 2, slot).start()
         return carry
 
-    lax.fori_loop(0, raw_steps, raw_body, 0)
+    part_one, part_two = raw_steps // 2, raw_steps - raw_steps // 3
+    lax.fori_loop(0, part_one, raw_body, 0)
 
     scale = HEAD ** -0.5
     causal = (lax.broadcasted_iota(jnp.int32, (tokens, tokens), 0) <= lax.broadcasted_iota(jnp.int32, (tokens, tokens), 1))
@@ -269,15 +298,29 @@
         one, two = v[0:HALF], v[HALF:HEAD]
         return jnp.concatenate([one * cos_t + two * sin_t, two * cos_t - one * sin_t], axis=0).astype(BF)
 
-    def attn_body(j, carry):
-        @pl.when(j == heads - 1)
+    last = half_heads - 1
+
+    def head_rows(j):
+        base = pl.multiple_of(j * GROUP, 32)
+        return tuple(pl.ds(base + n * HEAD, HEAD) for n in range(3))
+
+    def probabilities(j, q, k):
+        scores = jnp.where(causal, dot_tn(k, q) * scale, -1e30)
+        weight = jnp.exp(scores - jnp.max(scores, axis=0, keepdims=True))
+        prob = weight / jnp.sum(weight, axis=0, keepdims=True)
+        late_ref[j] = prob[:, rows:]
+        early_ref[j] = prob[0:rows, 0:rows]
+        return prob
+
+    def attn_body(i, carry):
+        j = mine(i)
+
+        @pl.when(i == last)
         def _():
-            qkv_copy(j).wait_send()
-            for n in range(1, 5):
-                ga_copy(n).start()
+            qkv_copy(theirs(i)).wait_send()
+            ga_copy(1).start()
         qkv_copy(j).wait_recv()
-        base = pl.multiple_of(j * GROUP, 32)
-        r_q, r_k, r_v = (pl.ds(base + n * HEAD, HEAD) for n in range(3))
+        r_q, r_k, r_v = head_rows(j)
         cos_t, sin_t = cos_ref[...], sin_ref[...]
         q = rope(add_bf(qkv_send[r_q, :], qkv_recv[r_q, :]), cos_t, sin_t)
         k = rope(add_bf(qkv_send[r_k, :], qkv_recv[r_k, :]), cos_t, sin_t)
@@ -285,15 +328,17 @@
         rot_ref[r_q, :] = q
         rot_ref[r_k, :] = k
         rot_ref[r_v, :] = v
-        scores = jnp.where(causal, dot_tn(k, q) * scale, -1e30)
-        weight = jnp.exp(scores - jnp.max(scores, axis=0, keepdims=True))
-        prob = weight / jnp.sum(weight, axis=0, keepdims=True)
-        late_ref[j] = prob[:, rows:]
-        early_ref[j] = prob[0:rows, 0:rows]
-        mix_ref[pl.ds(pl.multiple_of(j * HEAD, 32), HEAD), :] = dot_nn(v, prob.astype(BF)).astype(BF)
-        return carry
-
-    lax.fori_loop(0, heads, attn_body, 0)
+        prob = probabilities(j, q, k)
+        mix_ref[mix_rows(j), :] = dot_nn(v, prob.astype(BF)).astype(BF)
+        mix_copy(j).start()
+        return carry
+
+    lax.fori_loop(0, half_heads, attn_body, 0)
+    for n in range(2, 6):
+        ga_copy(n).start()
+    lax.fori_loop(part_one, part_two, raw_body, 0)
+    for i in range(half_heads):
+        mix_copy(theirs(i)).wait_recv()
     stores.append(store(mix_ref, mix_hbm, 1))
 
     loads[4].wait()
@@ -332,19 +377,20 @@
 
         lax.fori_loop(0, GU_PIECES, gu_body, 0)
 
-    stage2(AR_OUT, 1)
-    p2_copy(AR_OUT, 1).wait_send()
-    stage2(AR_OUT, 0)
-    stage3(AR_OUT, 1)
-    hidden_fwd(1)
-    for k in range(5, 8):
+    stage2(AR_OUT, LATE)
+    lax.fori_loop(part_two, raw_steps, raw_body, 0)
+    p2_copy(AR_OUT, LATE).wait_send()
+    stage2(AR_OUT, EARLY)
+    stage3(AR_OUT, LATE)
+    hidden_fwd(LATE)
+    for k in range(6, 8):
         ga_copy(k).start()
-    gate_up(1, 2)
-    stage3(AR_OUT, 0)
-    hidden_fwd(0)
-    gu_start(1, 2)
-    gu_start(1, 3)
-    gate_up(0, 0)
+    gate_up(LATE, 2)
+    stage3(AR_OUT, EARLY)
+    hidden_fwd(EARLY)
+    gu_start(LATE, 2)
+    gu_start(LATE, 3)
+    gate_up(EARLY, 0)
     tile = 512
     stores.append(store(r2_ref, r2_hbm, 2))
 
@@ -353,7 +399,7 @@
     for c in order:
         p1_copy(AR_OUT, c).wait_send()
         p3_copy(AR_OUT, c).wait_send()
-    p2_copy(AR_OUT, 0).wait_send()
+    p2_copy(AR_OUT, EARLY).wait_send()
 
     def mlp_pieces(c, lo, hi, then_at=None):
         r = pl.ds(c * rows, rows)
@@ -366,7 +412,7 @@
             if then_at is not None:
                 @pl.when(q == then_at)
                 def _():
-                    gu_start(0, 0)
+                    gu_start(EARLY, 0)
             for n in range(gu_cols // 256):
                 cg = pl.ds(pl.multiple_of(q * gu_cols + n * 256, 256), 256)
                 cu = pl.ds(pl.multiple_of(ff + q * gu_cols + n * 256, 256), 256)
@@ -433,10 +479,9 @@
         weighted = prob * dp
         return ((weighted - prob * jnp.sum(weighted, axis=0, keepdims=True)) * scale).astype(BF)
 
-    def late_body(j, carry):
-        base = pl.multiple_of(j * GROUP, 32)
-        r_q, r_k, r_v = (pl.ds(base + n * HEAD, HEAD) for n in range(3))
-        r_a = pl.ds(pl.multiple_of(j * HEAD, 32), HEAD)
+    def late_head(j):
+        r_q, r_k, r_v = head_rows(j)
+        r_a = mix_rows(j)
         cos_t, sin_t = cos_ref[:, rows:], sin_ref[:, rows:]
         da = add_bf(gm_send[r_a, rows:], gm_recv[r_a, rows:])
         prob = late_ref[j]
@@ -449,12 +494,22 @@
         dqkv_ref[r_v, rows:] = dv[:, rows:].astype(BF)
         kv_part[0, r_a, :] = dk[:, 0:rows]
         kv_part[1, r_a, :] = dv[:, 0:rows]
+
+    def late_mine(i, carry):
+        late_head(mine(i))
+        return carry
+
+    def late_theirs(i, carry):
+        j = theirs(i)
+        rot_copy(j).wait_recv()
+        r_q, r_k, _ = head_rows(j)
+        probabilities(j, rot_ref[r_q, :], rot_ref[r_k, :])
+        late_head(j)
         return carry
 
     def early_body(j, carry):
-        base = pl.multiple_of(j * GROUP, 32)
-        r_q, r_k, r_v = (pl.ds(base + n * HEAD, HEAD) for n in range(3))
-        r_a = pl.ds(pl.multiple_of(j * HEAD, 32), HEAD)
+        r_q, r_k, r_v = head_rows(j)
+        r_a = mix_rows(j)
         cos_t, sin_t = cos_ref[:, 0:rows], sin_ref[:, 0:rows]
         da = add_bf(gm_send[r_a, 0:rows], gm_recv[r_a, 0:rows])
         prob = early_ref[j]
@@ -466,10 +521,7 @@
         dqkv_ref[r_v, 0:rows] = dv.astype(BF)
         return carry
 
-    def attn_back(c):
-        for hf in range(2):
-            gm_copy(c, hf).wait_recv()
-            lax.fori_loop(hf * heads // 2, (hf + 1) * heads // 2, late_body if c else early_body, 0)
+    def input_cot(c):
         r = pl.ds(c * rows, rows)
         cot = dot_tn(dqkv_ref[:, c * rows:(c + 1) * rows], wqkv_ref[...])
         part_ref[SLOT[AR_R1], r, :] = cot.astype(BF)
@@ -490,43 +542,55 @@
         dg1_ref[...] += jnp.sum(gin * unit, axis=0, keepdims=True)
 
     def rest_of_gate_up():
-        gu_start(0, 2)
-        gu_start(0, 3)
-
-    mlp_pieces(1, 0, 4, then_at=2)
-    mlp_end(1)
-    gu_start(0, 1)
-    stage2(AR_R2, 1)
-    down_chunk(1)
-    stage3(AR_R2, 1)
-    stage2(AR_Y, 1)
-    hidden_back(1, rest_of_gate_up)
-    mlp_pieces(0, 0, 2)
-    stage3(AR_Y, 1)
-    attn_back(1)
-    mlp_pieces(0, 2, 3)
-    stage2(AR_R1, 1)
-    mlp_pieces(0, 3, 4)
-    mlp_end(0)
+        gu_start(EARLY, 2)
+        gu_start(EARLY, 3)
+        for i in range(2):
+            rot_copy(mine(i)).start()
+
+    mlp_pieces(LATE, 0, GU_PIECES, then_at=2)
+    mlp_end(LATE)
+    gu_start(EARLY, 1)
+    stage2(AR_R2, LATE)
+    down_chunk(LATE)
+    stage3(AR_R2, LATE)
+    stage2(AR_Y, LATE)
+    hidden_back(LATE, rest_of_gate_up)
+    mlp_pieces(EARLY, 0, 2)
+    stage3(AR_Y, LATE)
+    gm_copy(LATE, emb).wait_recv()
+    lax.fori_loop(0, half_heads, late_mine, 0)
+    y_chunk(LATE)
+    mlp_pieces(EARLY, 2, GU_PIECES)
+    mlp_end(EARLY)
+    for i in range(2, half_heads):
+        rot_copy(mine(i)).start()
     stores.append(store(dgu_ref, dgu_hbm, 3))
     stores.append(store(act_ref, act_hbm, 4))
-    stage2(AR_R2, 0)
-    down_chunk(0)
-    stage3(AR_R1, 1)
-    y_chunk(1)
-    stage3(AR_R2, 0)
-    hidden_back(0)
+    stage2(AR_R2, EARLY)
+    down_chunk(EARLY)
+    gm_copy(LATE, 1 - emb).wait_recv()
+    lax.fori_loop(0, 2, late_theirs, 0)
+    stage3(AR_R2, EARLY)
+    hidden_back(EARLY)
     stores.append(store(dh_ref, dh_hbm, 5))
-    stage2(AR_Y, 0)
-    input_back(1)
-    attn_back(0)
+    stage2(AR_Y, EARLY)
+    lax.fori_loop(2, half_heads, late_theirs, 0)
+    input_cot(LATE)
+    gm_copy(EARLY, 0).wait_recv()
+    stage2(AR_R1, LATE)
+    lax.fori_loop(0, half_heads, early_body, 0)
+    gm_copy(EARLY, 1).wait_recv()
+    lax.fori_loop(half_heads, heads, early_body, 0)
+    input_cot(EARLY)
     stores.append(store(dqkv_ref, dqkv_hbm, 7))
-    stage2(AR_R1, 0)
-    stage3(AR_Y, 0)
-    y_chunk(0)
+    stage3(AR_R1, LATE)
+    stage2(AR_R1, EARLY)
+    stage3(AR_Y, EARLY)
+    input_back(LATE)
+    y_chunk(EARLY)
     stores.append(store(h_ref, y_hbm, 6))
-    stage3(AR_R1, 0)
-    input_back(0)
+    stage3(AR_R1, EARLY)
+    input_back(EARLY)
 
     for k in range(3):
         stat_copy(k).wait_send()
@@ -535,8 +599,11 @@
             dots_copy(k, n).wait_send()
     for k in range(8):
         ga_copy(k).wait_send()
-    for j in range(heads - 1):
-        qkv_copy(j).wait_send()
+    for i in range(half_heads):
+        if i < last:
+            qkv_copy(theirs(i)).wait_send()
+        mix_copy(mine(i)).wait_send()
+        rot_copy(mine(i)).wait_send()
     for c in range(CHUNKS):
         for q in range(GU_PIECES):
             for k in range(2):
@@ -585,7 +652,8 @@
     ]
     for n in (3, 8, heads, 2 * GU_PIECES * CHUNKS, 2 * CHUNKS, 4 * CHUNKS, 4 * CHUNKS, 4 * CHUNKS):
         scratch += [pltpu.SemaphoreType.DMA((n,)), pltpu.SemaphoreType.DMA((n,))]
-    scratch += [pltpu.SemaphoreType.DMA((7 * 2 * CHUNKS,)), pltpu.SemaphoreType.DMA((8 * 2 * CHUNKS,))]
+    for n in (7 * 2 * CHUNKS, 8 * 2 * CHUNKS, heads, heads, heads, heads):
+        scratch += [pltpu.SemaphoreType.DMA((n,))]
     vec = jax.ShapeDtypeStruct((1, width), F32)
     return pl.pallas_call(
         layer_kernel,
@@ -609,7 +677,7 @@
     pairs = [(dqkv_hbm, dqkv_ref), (r1_hbm, r1_ref), (r2_hbm, r2_ref), (dgu_hbm, dgu_ref), (mix_hbm, mix_ref), (dh_hbm, dh_ref),
              (act_hbm, act_ref), (dy_hbm, dy_ref), (y_in, y_ref), (dx_in, dx_ref)]
     loads = [pltpu.make_async_copy(src, dst, load_sem.at[n]) for n, (src, dst) in enumerate(pairs)]
-    for copy in loads:
+    for copy in loads[:2]:
         copy.start()
     dg1_out[...] = dg1_in[...].reshape(dg1_out.shape)
     dg2_out[...] = dg2_in[...].reshape(dg2_out.shape)
@@ -638,6 +706,8 @@
 
     loads[0].wait()
     loads[1].wait()
+    for copy in loads[2:]:
+        copy.start()
     sent = product(qkv_out, plain_rows(dqkv_ref), r1_ref, 0)
 
     loads[2].wait()
@@ -650,9 +720,9 @@
     gu_steps = gu_out.shape[0] // GU_BLOCK
 
     def gu_body(i, carry):
-        slot = lax.rem(i, 2)
-
-        @pl.when(i >= 2)
+        slot = lax.rem(i, slots)
+
+        @pl.when(i >= slots)
         def _():
             inter_copy(0, slot).wait()
         lhs = r2_ref[:, step(i, GU_BLOCK)].T
@@ -680,7 +750,6 @@
         copy.start()
     for slot in range(slots):
         rows_copy(down_out, 0, slot).wait()
-    for slot in range(2):
         inter_copy(0, slot).wait()
     for copy in ends:
         copy.wait()
@@ -704,8 +773,8 @@
         out_specs=[any_spec] * 6 + [vmem_spec] * 2,
         out_shape=[out(ff, width), out(width, 32, 128), out(mix.shape[0], width), out(dqkv.shape[0], width), like(y), like(dx), out(width), out(width)],
         scratch_shapes=[pltpu.VMEM(a.shape, a.dtype) for a in arrays] + [
-            pltpu.VMEM((4, 256, width), F32), pltpu.VMEM((2, GU_BLOCK * 40, 128), F32),
-            pltpu.SemaphoreType.DMA((10,)), pltpu.SemaphoreType.DMA((4,)), pltpu.SemaphoreType.DMA((2,)), pltpu.SemaphoreType.DMA((2,))],
+            pltpu.VMEM((4, 256, width), F32), pltpu.VMEM((4, GU_BLOCK * 40, 128), F32),
+            pltpu.SemaphoreType.DMA((10,)), pltpu.SemaphoreType.DMA((4,)), pltpu.SemaphoreType.DMA((4,)), pltpu.SemaphoreType.DMA((2,))],
         compiler_params=pltpu.CompilerParams(vmem_limit_bytes=56 << 20),
     )(*arrays, dg1, dg2)
 

time: 169 us -> 159 us (0.941)
  Pallas kernels: 167 us -> 157 us
    pallas_call x1, Pallas kernels: 142 us -> 134 us  [run_layer(): pl.pallas_call(layer_kernel, name='layer', out_shape=(act(width), act(wid...]
    pallas_call x1, Pallas kernels: 25.4 us -> 23.2 us  [weight_grads(): pl.pallas_call(grads_kernel, name='weight_grads', in_specs=[any_spec] * 1...]
where the time goes in v5:
time: 159 us; the launch traced here: 158 us
  Pallas kernels  157 us (99%)
    pallas_call x1, Pallas kernels, run_layer(): pl.pallas_call(layer_kernel, name='layer', out_shape=(act(width), act(wid...  134 us
    pallas_call x1, Pallas kernels, weight_grads(): pl.pallas_call(grads_kernel, name='weight_grads', in_specs=[any_spec] * 1...  23.2 us

profile of v5, /device:TPU:0, one launch (start us, length us, event | category | flops | bytes accessed | tf_op | source)
XLA Modules:
  0.0 158.2 jit_solution(8368469641494174071)
XLA Ops:
  0.6 134.2 %layer.1 = (bf16[256,1536]{1,0:T(8,128)(2,1)}, bf16[256,1536]{1,0:T(8,128)(2,1)}, f32[1,1536]{1,0:T(1,128)}, f32[1,1536]{1,0:T(1,128)}, bf16[256,1536]{1,0:T(8,1...) custom-call(bf16[256,1536]{1,0:T(8,128)(2,1)} %x_hbm.1, ...), custom_call_target="tpu_custom_call" | custom-call | tf_op jit(solution)/shard_map/layer/pallas_call | solution.py:658
  134.8 23.2 %weight_grads.1 = (f32[2048,1536]{1,0:T(8,128)}, f32[1536,32,128]{2,1,0:T(8,128)}, f32[768,1536]{1,0:T(8,128)}, f32[2304,1536]{1,0:T(8,128)}, bf16[256,1536]{1,0...) custom-call(bf16[256,2048]{1,0:T(8,128)(2,1)} %get-tuple-element.27.act_hbm, ...), custom_call_target="tpu_custom_call" | custom-call | tf_op jit(solution)/shard_map/weight_grads/pallas_call | solution.py:769

commit v6 on v5

--- a/solution.py
+++ b/solution.py
@@ -44,10 +44,10 @@
 
 
 def layer_kernel(x_hbm, dy_hbm, g1_in, g2_in, pos_in, wqkv_hbm, wout_hbm, wgu_hbm, wdown_hbm,
-                 y_hbm, dx_hbm, dg1_ref, dg2_ref, r1_hbm, dqkv_hbm, mix_hbm, dh_hbm, r2_hbm, dgu_hbm, act_hbm,
+                 y_hbm, dx_hbm, dg1_hbm, dg2_hbm, r1_hbm, dqkv_hbm, mix_hbm, dh_hbm, r2_hbm, dgu_hbm, act_hbm,
                  x_ref, dy_ref, wqkv_ref, wout_ref, wg_ref, wu_ref, wdown_ref, raw_ref,
                  g1_ref, g2_ref, cos_ref, sin_ref, r1_ref, r2_ref, h_ref, dh_ref, act_ref, dgu_ref, rot_ref, late_ref, early_ref, mix_ref, dqkv_ref, dx_ref,
-                 kv_part, cot_ref, dots_ref,
+                 kv_part, cot_ref, dots_ref, dg1_ref, dg2_ref,
                  inv1_ref, inv2_ref,
                  ga_send, ga_recv, qkv_send, qkv_recv, gu_send, gu_recv, gm_send, gm_recv, stat_send, stat_recv,
                  part_ref, sib_ref, half_ref, far_ref, full_ref,
@@ -401,16 +401,23 @@
         p3_copy(AR_OUT, c).wait_send()
     p2_copy(AR_OUT, EARLY).wait_send()
 
-    def mlp_pieces(c, lo, hi, then_at=None):
+    def mlp_pieces(c, lo, hi):
         r = pl.ds(c * rows, rows)
         if lo == 0:
             cot_ref[...] = jnp.zeros_like(cot_ref)
 
         def piece(q, carry):
+            if c == EARLY:
+                @pl.when(q == GU_PIECES - 1)
+                def _():
+                    for k in range(2):
+                        gu_copy(c, q, k).wait_send()
+                    for i in range(2):
+                        rot_copy(mine(i)).start()
             gu_copy(c, q, 0).wait_recv()
             gu_copy(c, q, 1).wait_recv()
-            if then_at is not None:
-                @pl.when(q == then_at)
+            if c == LATE:
+                @pl.when(q == 2)
                 def _():
                     gu_start(EARLY, 0)
             for n in range(gu_cols // 256):
@@ -479,24 +486,31 @@
         weighted = prob * dp
         return ((weighted - prob * jnp.sum(weighted, axis=0, keepdims=True)) * scale).astype(BF)
 
-    def late_head(j):
-        r_q, r_k, r_v = head_rows(j)
-        r_a = mix_rows(j)
+    def write(stored):
+        for ref, at, value in stored:
+            ref[at] = value
+
+    def late_heads(js):
+        stored = []
         cos_t, sin_t = cos_ref[:, rows:], sin_ref[:, rows:]
-        da = add_bf(gm_send[r_a, rows:], gm_recv[r_a, rows:])
-        prob = late_ref[j]
-        k = rot_ref[r_k, :]
-        ds = scores_back(rot_ref[r_v, :], da, prob)
-        dv = dot_nt(da, prob.astype(BF))
-        dk = dot_nt(rot_ref[r_q, rows:], ds)
-        dqkv_ref[r_q, rows:] = unrope(dot_nn(k, ds).astype(BF), cos_t, sin_t)
-        dqkv_ref[r_k, rows:] = unrope(dk[:, rows:].astype(BF), cos_t, sin_t)
-        dqkv_ref[r_v, rows:] = dv[:, rows:].astype(BF)
-        kv_part[0, r_a, :] = dk[:, 0:rows]
-        kv_part[1, r_a, :] = dv[:, 0:rows]
+        late, early = slice(rows, None), slice(0, rows)
+        for j in js:
+            r_q, r_k, r_v = head_rows(j)
+            r_a = mix_rows(j)
+            da = add_bf(gm_send[r_a, late], gm_recv[r_a, late])
+            prob = late_ref[j]
+            k = rot_ref[r_k, :]
+            ds = scores_back(rot_ref[r_v, :], da, prob)
+            dv = dot_nt(da, prob.astype(BF))
+            dk = dot_nt(rot_ref[r_q, late], ds)
+            stored += [(dqkv_ref, (r_q, late), unrope(dot_nn(k, ds).astype(BF), cos_t, sin_t)),
+                       (dqkv_ref, (r_k, late), unrope(dk[:, late].astype(BF), cos_t, sin_t)),
+                       (dqkv_ref, (r_v, late), dv[:, late].astype(BF)),
+                       (kv_part, (0, r_a), dk[:, early]), (kv_part, (1, r_a), dv[:, early])]
+        write(stored)
 
     def late_mine(i, carry):
-        late_head(mine(i))
+        late_heads((mine(2 * i), mine(2 * i + 1)))
         return carry
 
     def late_theirs(i, carry):
@@ -504,26 +518,35 @@
         rot_copy(j).wait_recv()
         r_q, r_k, _ = head_rows(j)
         probabilities(j, rot_ref[r_q, :], rot_ref[r_k, :])
-        late_head(j)
+        late_heads((j,))
         return carry
 
-    def early_body(j, carry):
-        r_q, r_k, r_v = head_rows(j)
-        r_a = mix_rows(j)
-        cos_t, sin_t = cos_ref[:, 0:rows], sin_ref[:, 0:rows]
-        da = add_bf(gm_send[r_a, 0:rows], gm_recv[r_a, 0:rows])
-        prob = early_ref[j]
-        ds = scores_back(rot_ref[r_v, 0:rows], da, prob)
-        dv = kv_part[1, r_a, :] + dot_nt(da, prob.astype(BF))
-        dk = kv_part[0, r_a, :] + dot_nt(rot_ref[r_q, 0:rows], ds)
-        dqkv_ref[r_q, 0:rows] = unrope(dot_nn(rot_ref[r_k, 0:rows], ds).astype(BF), cos_t, sin_t)
-        dqkv_ref[r_k, 0:rows] = unrope(dk.astype(BF), cos_t, sin_t)
-        dqkv_ref[r_v, 0:rows] = dv.astype(BF)
+    def early_body(i, carry):
+        stored = []
+        early = slice(0, rows)
+        cos_t, sin_t = cos_ref[:, early], sin_ref[:, early]
+        for j in (2 * i, 2 * i + 1):
+            r_q, r_k, r_v = head_rows(j)
+            r_a = mix_rows(j)
+            da = add_bf(gm_send[r_a, early], gm_recv[r_a, early])
+            prob = early_ref[j]
+            ds = scores_back(rot_ref[r_v, early], da, prob)
+            dv = kv_part[1, r_a, :] + dot_nt(da, prob.astype(BF))
+            dk = kv_part[0, r_a, :] + dot_nt(rot_ref[r_q, early], ds)
+            stored += [(dqkv_ref, (r_q, early), unrope(dot_nn(rot_ref[r_k, early], ds).astype(BF), cos_t, sin_t)),
+                       (dqkv_ref, (r_k, early), unrope(dk.astype(BF), cos_t, sin_t)),
+                       (dqkv_ref, (r_v, early), dv.astype(BF))]
+        write(stored)
         return carry
 
+    half_chans = half_heads * GROUP
+
+    def cot_product(c, lo, hi):
+        return dot_tn(dqkv_ref[lo:hi, c * rows:(c + 1) * rows], wqkv_ref[lo:hi, :])
+
     def input_cot(c):
         r = pl.ds(c * rows, rows)
-        cot = dot_tn(dqkv_ref[:, c * rows:(c + 1) * rows], wqkv_ref[...])
+        cot = cot_product(c, half_chans, None) + (cot_ref[...] if c == EARLY else cot_product(c, 0, half_chans))
         part_ref[SLOT[AR_R1], r, :] = cot.astype(BF)
         p1_copy(AR_R1, c).start()
         unit = x_ref[r, :].astype(F32) * inv1_ref[r, :]
@@ -544,10 +567,8 @@
     def rest_of_gate_up():
         gu_start(EARLY, 2)
         gu_start(EARLY, 3)
-        for i in range(2):
-            rot_copy(mine(i)).start()
-
-    mlp_pieces(LATE, 0, GU_PIECES, then_at=2)
+
+    mlp_pieces(LATE, 0, GU_PIECES)
     mlp_end(LATE)
     gu_start(EARLY, 1)
     stage2(AR_R2, LATE)
@@ -558,7 +579,7 @@
     mlp_pieces(EARLY, 0, 2)
     stage3(AR_Y, LATE)
     gm_copy(LATE, emb).wait_recv()
-    lax.fori_loop(0, half_heads, late_mine, 0)
+    lax.fori_loop(0, half_heads // 2, late_mine, 0)
     y_chunk(LATE)
     mlp_pieces(EARLY, 2, GU_PIECES)
     mlp_end(EARLY)
@@ -573,24 +594,27 @@
     stage3(AR_R2, EARLY)
     hidden_back(EARLY)
     stores.append(store(dh_ref, dh_hbm, 5))
+    stores.append(store(dg2_ref, dg2_hbm, 6))
     stage2(AR_Y, EARLY)
     lax.fori_loop(2, half_heads, late_theirs, 0)
     input_cot(LATE)
     gm_copy(EARLY, 0).wait_recv()
     stage2(AR_R1, LATE)
-    lax.fori_loop(0, half_heads, early_body, 0)
+    lax.fori_loop(0, half_heads // 2, early_body, 0)
+    cot_ref[...] = cot_product(EARLY, 0, half_chans)
     gm_copy(EARLY, 1).wait_recv()
-    lax.fori_loop(half_heads, heads, early_body, 0)
+    lax.fori_loop(half_heads // 2, half_heads, early_body, 0)
     input_cot(EARLY)
     stores.append(store(dqkv_ref, dqkv_hbm, 7))
+    stage2(AR_R1, EARLY)
     stage3(AR_R1, LATE)
-    stage2(AR_R1, EARLY)
     stage3(AR_Y, EARLY)
     input_back(LATE)
     y_chunk(EARLY)
-    stores.append(store(h_ref, y_hbm, 6))
+    stores.append(store(h_ref, y_hbm, 10))
     stage3(AR_R1, EARLY)
     input_back(EARLY)
+    stores.append(store(dg1_ref, dg1_hbm, 11))
 
     for k in range(3):
         stat_copy(k).wait_send()
@@ -605,7 +629,7 @@
         mix_copy(mine(i)).wait_send()
         rot_copy(mine(i)).wait_send()
     for c in range(CHUNKS):
-        for q in range(GU_PIECES):
+        for q in range(GU_PIECES - (c == EARLY)):
             for k in range(2):
                 gu_copy(c, q, k).wait_send()
         for hf in range(2):
@@ -639,7 +663,7 @@
         pltpu.VMEM((tokens, ff), BF), pltpu.VMEM((tokens, 2 * ff), BF),
         pltpu.VMEM((chans, tokens), BF), pltpu.VMEM((heads, tokens, rows), F32), pltpu.VMEM((heads, rows, rows), F32), pltpu.VMEM((mix, tokens), BF), pltpu.VMEM((chans, tokens), BF),
         pltpu.VMEM((tokens, width), BF),
-        pltpu.VMEM((2, mix, rows), F32), pltpu.VMEM((rows, width), F32), pltpu.VMEM((2 * CHUNKS, 8, 8, rows), F32),
+        pltpu.VMEM((2, mix, rows), F32), pltpu.VMEM((rows, width), F32), pltpu.VMEM((2 * CHUNKS, 8, 8, rows), F32), pltpu.VMEM((1, width), F32), pltpu.VMEM((1, width), F32),
         pltpu.VMEM((tokens, 1), F32), pltpu.VMEM((tokens, 1), F32),
         pltpu.VMEM((tokens, ff), BF), pltpu.VMEM((tokens, ff), BF),
         pltpu.VMEM((chans, tokens), BF), pltpu.VMEM((chans, tokens), BF),
@@ -648,7 +672,7 @@
         pltpu.VMEM((3, 8, tokens), F32), pltpu.VMEM((3, 8, tokens), F32),
         pltpu.VMEM((3, tokens, width), BF), pltpu.VMEM((3, tokens, width // 2), BF), pltpu.VMEM((3, tokens, width // 2), BF),
         pltpu.VMEM((3, tokens, width // 2), BF), pltpu.VMEM((3, tokens, width), BF),
-        pltpu.SemaphoreType.DMA((5,)), pltpu.SemaphoreType.DMA((2,)), pltpu.SemaphoreType.DMA((8 + CHUNKS,)),
+        pltpu.SemaphoreType.DMA((5,)), pltpu.SemaphoreType.DMA((2,)), pltpu.SemaphoreType.DMA((10 + CHUNKS,)),
     ]
     for n in (3, 8, heads, 2 * GU_PIECES * CHUNKS, 2 * CHUNKS, 4 * CHUNKS, 4 * CHUNKS, 4 * CHUNKS):
         scratch += [pltpu.SemaphoreType.DMA((n,)), pltpu.SemaphoreType.DMA((n,))]
@@ -661,7 +685,7 @@
         out_shape=(act(width), act(width), vec, vec, act(width), jax.ShapeDtypeStruct((chans, tokens), BF),
                    jax.ShapeDtypeStruct((mix, tokens), BF), act(width), act(width), act(2 * ff), act(ff)),
         in_specs=[any_spec, any_spec, vmem_spec, vmem_spec, vmem_spec, any_spec, any_spec, any_spec, any_spec],
-        out_specs=(any_spec, any_spec, vmem_spec, vmem_spec) + (any_spec,) * 7,
+        out_specs=(any_spec,) * 11,
         scratch_shapes=scratch,
         compiler_params=pltpu.CompilerParams(collective_id=0, has_side_effects=True, vmem_limit_bytes=67000000),
     )(x_in, grad_out, gain_one, gain_two, positions, w_qkv, w_out, w_gu, w_down)

time: 159 us -> 157 us (0.987)
  no operation moved by 1% of the time
where the time goes in v6:
time: 157 us
  Pallas kernels  156 us (99%)
    pallas_call x1, Pallas kernels, run_layer(): pl.pallas_call(layer_kernel, name='layer', out_shape=(act(width), act(wid...  133 us
    pallas_call x1, Pallas kernels, weight_grads(): pl.pallas_call(grads_kernel, name='weight_grads', in_specs=[any_spec] * 1...  23.2 us

profile of v6, /device:TPU:0, one launch (start us, length us, event | category | flops | bytes accessed | tf_op | source)
XLA Modules:
  0.0 156.7 jit_solution(10188430120927970148)
XLA Ops:
  0.6 132.7 %layer.1 = (bf16[256,1536]{1,0:T(8,128)(2,1)}, bf16[256,1536]{1,0:T(8,128)(2,1)}, f32[1,1536]{1,0:T(1,128)}, f32[1,1536]{1,0:T(1,128)}, bf16[256,1536]{1,0:T(8,1...) custom-call(bf16[256,1536]{1,0:T(8,128)(2,1)} %x_hbm.1, ...), custom_call_target="tpu_custom_call" | custom-call | tf_op jit(solution)/shard_map/layer/pallas_call | solution.py:682
  133.4 23.2 %weight_grads.1 = (f32[2048,1536]{1,0:T(8,128)}, f32[1536,32,128]{2,1,0:T(8,128)}, f32[768,1536]{1,0:T(8,128)}, f32[2304,1536]{1,0:T(8,128)}, bf16[256,1536]{1,0...) custom-call(bf16[256,2048]{1,0:T(8,128)(2,1)} %get-tuple-element.27.act_hbm, ...), custom_call_target="tpu_custom_call" | custom-call | tf_op jit(solution)/shard_map/weight_grads/pallas_call | solution.py:793

commit v7 on v6

--- a/solution.py
+++ b/solution.py
@@ -101,13 +101,16 @@
 
     def ga_copy(k):
         cols = step(k, ga_cols)
-        return send(ga_send.at[:, cols], ga_recv.at[:, cols], ga_s.at[k], ga_r.at[k], partner)
-
-    def qkv_copy(j):
+        return send(ga_send.at[:, cols], ga_recv.at[:, cols], ga_s.at[0], ga_r.at[0], partner)
+
+    ga_all = send(ga_send, ga_recv, ga_s.at[0], ga_r.at[0], partner)
+
+    def qkv_copy(i, j):
         r = step(j, GROUP)
-        return send(qkv_send.at[r], qkv_recv.at[r], qk_s.at[j], qk_r.at[j], partner)
+        return send(qkv_send.at[r], qkv_recv.at[r], qk_s.at[0], qk_r.at[i], partner)
 
     half_heads = heads // 2
+    half_chans = half_heads * GROUP
 
     def mine(i):
         return emb * half_heads + i
@@ -120,24 +123,35 @@
 
     def mix_copy(j):
         at = mix_ref.at[mix_rows(j)]
-        return send(at, at, mx_s.at[j], mx_r.at[j], partner)
-
-    def rot_copy(j):
+        return send(at, at, mx_s.at[0], mx_r.at[0], partner)
+
+    def mix_all(which):
+        at = mix_ref.at[step(which, half_heads * HEAD)]
+        return send(at, at, mx_s.at[0], mx_r.at[0], partner)
+
+    def rot_copy(i, j):
         at = rot_ref.at[step(j, GROUP)]
-        return send(at, at, rt_s.at[j], rt_r.at[j], partner)
+        return send(at, at, rt_s.at[0], rt_r.at[i], partner)
 
     gu_cols = ff // GU_PIECES
 
     def gu_copy(c, q, k):
         at = (pl.ds(c * rows, rows), pl.ds(pl.multiple_of(k * ff + q * gu_cols, gu_cols), gu_cols))
-        n = (c * GU_PIECES + q) * 2 + k
-        return send(gu_send.at[at], gu_recv.at[at], gu_s.at[n], gu_r.at[n], partner)
+        return send(gu_send.at[at], gu_recv.at[at], gu_s.at[c], gu_r.at[c * GU_PIECES + q], partner)
+
+    def gu_pair(c, q):
+        at = (pl.ds(c * rows, rows), pl.ds(0, 2 * gu_cols))
+        return send(gu_send.at[at], gu_recv.at[at], gu_s.at[c], gu_r.at[c * GU_PIECES + q], partner)
+
+    def gu_sent(c):
+        at = pl.ds(c * rows, rows)
+        send(gu_send.at[at], gu_recv.at[at], gu_s.at[c], gu_r.at[0], partner).wait_send()
 
     gm_rows = gm_send.shape[0] // 2
 
     def gm_copy(c, hf):
         at = (step(hf, gm_rows), pl.ds(c * rows, rows))
-        return send(gm_send.at[at], gm_recv.at[at], gm_s.at[2 * c + hf], gm_r.at[2 * c + hf], partner)
+        return send(gm_send.at[at], gm_recv.at[at], gm_s.at[c], gm_r.at[2 * c + hf], partner)
 
     own = pl.ds(pl.multiple_of(core * half_width, half_width), half_width)
     other = pl.ds(pl.multiple_of((1 - core) * half_width, half_width), half_width)
@@ -145,7 +159,7 @@
     def p1_copy(i, c):
         r = pl.ds(c * rows, rows)
         k = i * CHUNKS + c
-        return send(part_ref.at[SLOT[i], r, other], sib_ref.at[SLOT[i], r], p1_s.at[k], p1_r.at[k], sibling)
+        return send(part_ref.at[SLOT[i], r, other], sib_ref.at[SLOT[i], r], p1_s.at[i], p1_r.at[k], sibling)
 
     def p2_copy(i, c):
         r = pl.ds(c * rows, rows)
@@ -155,7 +169,12 @@
     def p3_copy(i, c):
         r = pl.ds(c * rows, rows)
         k = i * CHUNKS + c
-        return send(full_ref.at[SLOT[i], r, own], full_ref.at[SLOT[i], r, own], p3_s.at[k], p3_r.at[k], sibling)
+        return send(full_ref.at[SLOT[i], r, own], full_ref.at[SLOT[i], r, own], p3_s.at[i], p3_r.at[k], sibling)
+
+    def p1_p3_sent(i):
+        n = SLOT[i]
+        send(part_ref.at[n, :, other], sib_ref.at[n], p1_s.at[i], p1_r.at[0], sibling).wait_send()
+        send(full_ref.at[n, :, own], full_ref.at[n, :, own], p3_s.at[i], p3_r.at[0], sibling).wait_send()
 
     def stage2(i, c):
         r = pl.ds(c * rows, rows)
@@ -186,7 +205,11 @@
 
     def dots_copy(k, n):
         at = dots_ref.at[k, me]
-        return send(at, at, dots_s.at[7 * k + n], dots_r.at[8 * k + me], others[n])
+        return send(at, at, dots_s.at[k], dots_r.at[k], others[n])
+
+    def dots_all(k):
+        at = dots_ref.at[k, pl.ds(0, 7)]
+        return send(at, at, dots_s.at[k], dots_r.at[k], partner)
 
     def dots_put(k, col):
         dots_ref[k, me] = jnp.broadcast_to(col, (rows, 128)).T[0:8, :]
@@ -194,10 +217,7 @@
             dots_copy(k, n).start()
 
     def dots_get(k):
-        for n in range(7):
-            src = lax.rem(emb + (n + 1) // 4, 2) * 4 + lax.rem(hid + n + 1, 4)
-            at = dots_ref.at[k, src]
-            send(at, at, dots_s.at[7 * k + n], dots_r.at[8 * k + src], others[n]).wait_recv()
+        dots_all(k).wait_recv()
         total = dots_ref[k, 0, 0:1, :]
         for n in range(1, 8):
             total = total + dots_ref[k, n, 0:1, :]
@@ -243,7 +263,7 @@
 
     def qkv_theirs(i, carry):
         qkv_product(theirs(i))
-        qkv_copy(theirs(i)).start()
+        qkv_copy(i, theirs(i)).start()
         return carry
 
     def qkv_mine(i, carry):
@@ -317,9 +337,10 @@
 
         @pl.when(i == last)
         def _():
-            qkv_copy(theirs(i)).wait_send()
+            r = step(1 - emb, half_chans)
+            send(qkv_send.at[r], qkv_recv.at[r], qk_s.at[0], qk_r.at[0], partner).wait_send()
             ga_copy(1).start()
-        qkv_copy(j).wait_recv()
+        qkv_copy(i, j).wait_recv()
         r_q, r_k, r_v = head_rows(j)
         cos_t, sin_t = cos_ref[...], sin_ref[...]
         q = rope(add_bf(qkv_send[r_q, :], qkv_recv[r_q, :]), cos_t, sin_t)
@@ -337,8 +358,7 @@
     for n in range(2, 6):
         ga_copy(n).start()
     lax.fori_loop(part_one, part_two, raw_body, 0)
-    for i in range(half_heads):
-        mix_copy(theirs(i)).wait_recv()
+    mix_all(1 - emb).wait_recv()
     stores.append(store(mix_ref, mix_hbm, 1))
 
     loads[4].wait()
@@ -394,11 +414,8 @@
     tile = 512
     stores.append(store(r2_ref, r2_hbm, 2))
 
-    for k in range(8):
-        ga_copy(k).wait_recv()
-    for c in order:
-        p1_copy(AR_OUT, c).wait_send()
-        p3_copy(AR_OUT, c).wait_send()
+    ga_all.wait_recv()
+    p1_p3_sent(AR_OUT)
     p2_copy(AR_OUT, EARLY).wait_send()
 
     def mlp_pieces(c, lo, hi):
@@ -410,12 +427,10 @@
             if c == EARLY:
                 @pl.when(q == GU_PIECES - 1)
                 def _():
-                    for k in range(2):
-                        gu_copy(c, q, k).wait_send()
+                    gu_sent(EARLY)
                     for i in range(2):
-                        rot_copy(mine(i)).start()
-            gu_copy(c, q, 0).wait_recv()
-            gu_copy(c, q, 1).wait_recv()
+                        rot_copy(i, mine(i)).start()
+            gu_pair(c, q).wait_recv()
             if c == LATE:
                 @pl.when(q == 2)
                 def _():
@@ -515,7 +530,7 @@
 
     def late_theirs(i, carry):
         j = theirs(i)
-        rot_copy(j).wait_recv()
+        rot_copy(i, j).wait_recv()
         r_q, r_k, _ = head_rows(j)
         probabilities(j, rot_ref[r_q, :], rot_ref[r_k, :])
         late_heads((j,))
@@ -539,8 +554,6 @@
         write(stored)
         return carry
 
-    half_chans = half_heads * GROUP
-
     def cot_product(c, lo, hi):
         return dot_tn(dqkv_ref[lo:hi, c * rows:(c + 1) * rows], wqkv_ref[lo:hi, :])
 
@@ -584,7 +597,7 @@
     mlp_pieces(EARLY, 2, GU_PIECES)
     mlp_end(EARLY)
     for i in range(2, half_heads):
-        rot_copy(mine(i)).start()
+        rot_copy(i, mine(i)).start()
     stores.append(store(dgu_ref, dgu_hbm, 3))
     stores.append(store(act_ref, act_hbm, 4))
     stage2(AR_R2, EARLY)
@@ -619,25 +632,19 @@
     for k in range(3):
         stat_copy(k).wait_send()
     for k in range(2 * CHUNKS):
-        for n in range(7):
-            dots_copy(k, n).wait_send()
-    for k in range(8):
-        ga_copy(k).wait_send()
-    for i in range(half_heads):
-        if i < last:
-            qkv_copy(theirs(i)).wait_send()
-        mix_copy(mine(i)).wait_send()
-        rot_copy(mine(i)).wait_send()
+        dots_all(k).wait_send()
+    ga_all.wait_send()
+    mix_all(emb).wait_send()
+    at = rot_ref.at[step(emb, half_chans)]
+    send(at, at, rt_s.at[0], rt_r.at[0], partner).wait_send()
     for c in range(CHUNKS):
-        for q in range(GU_PIECES - (c == EARLY)):
-            for k in range(2):
-                gu_copy(c, q, k).wait_send()
-        for hf in range(2):
-            gm_copy(c, hf).wait_send()
-        for i in range(1, 4):
-            p1_copy(i, c).wait_send()
+        at = (slice(None), pl.ds(c * rows, rows))
+        send(gm_send.at[at], gm_recv.at[at], gm_s.at[c], gm_r.at[0], partner).wait_send()
+        for i in (AR_R2, AR_Y, AR_R1):
             p2_copy(i, c).wait_send()
-            p3_copy(i, c).wait_send()
+    gu_sent(LATE)
+    for i in (AR_R2, AR_Y, AR_R1):
+        p1_p3_sent(i)
     for copy in stores:
         copy.wait()
 
@@ -674,9 +681,9 @@
         pltpu.VMEM((3, tokens, width // 2), BF), pltpu.VMEM((3, tokens, width), BF),
         pltpu.SemaphoreType.DMA((5,)), pltpu.SemaphoreType.DMA((2,)), pltpu.SemaphoreType.DMA((10 + CHUNKS,)),
     ]
-    for n in (3, 8, heads, 2 * GU_PIECES * CHUNKS, 2 * CHUNKS, 4 * CHUNKS, 4 * CHUNKS, 4 * CHUNKS):
-        scratch += [pltpu.SemaphoreType.DMA((n,)), pltpu.SemaphoreType.DMA((n,))]
-    for n in (7 * 2 * CHUNKS, 8 * 2 * CHUNKS, heads, heads, heads, heads):
+    half_heads = heads // 2
+    for n in (3, 3, 1, 1, 1, half_heads, CHUNKS, GU_PIECES * CHUNKS, CHUNKS, 2 * CHUNKS, 4, 4 * CHUNKS, 4 * CHUNKS, 4 * CHUNKS, 4, 4 * CHUNKS,
+              2 * CHUNKS, 2 * CHUNKS, 1, 1, 1, half_heads):
         scratch += [pltpu.SemaphoreType.DMA((n,))]
     vec = jax.ShapeDtypeStruct((1, width), F32)
     return pl.pallas_call(
@@ -706,7 +713,7 @@
     dg1_out[...] = dg1_in[...].reshape(dg1_out.shape)
     dg2_out[...] = dg2_in[...].reshape(dg2_out.shape)
 
-    slots = rows_ref.shape[0]
+    slots, inter_slots = rows_ref.shape[0], inter_ref.shape[0]
 
     def rows_copy(out, index, slot):
         return pltpu.make_async_copy(rows_ref.at[slot], out.at[step(index, block)], rows_sem.at[slot])
@@ -744,9 +751,9 @@
     gu_steps = gu_out.shape[0] // GU_BLOCK
 
     def gu_body(i, carry):
-        slot = lax.rem(i, slots)
-
-        @pl.when(i >= slots)
+        slot = lax.rem(i, inter_slots)
+
+        @pl.when(i >= inter_slots)
         def _():
             inter_copy(0, slot).wait()
         lhs = r2_ref[:, step(i, GU_BLOCK)].T
@@ -774,6 +781,7 @@
         copy.start()
     for slot in range(slots):
         rows_copy(down_out, 0, slot).wait()
+    for slot in range(inter_slots):
         inter_copy(0, slot).wait()
     for copy in ends:
         copy.wait()
@@ -797,8 +805,8 @@
         out_specs=[any_spec] * 6 + [vmem_spec] * 2,
         out_shape=[out(ff, width), out(width, 32, 128), out(mix.shape[0], width), out(dqkv.shape[0], width), like(y), like(dx), out(width), out(width)],
         scratch_shapes=[pltpu.VMEM(a.shape, a.dtype) for a in arrays] + [
-            pltpu.VMEM((4, 256, width), F32), pltpu.VMEM((4, GU_BLOCK * 40, 128), F32),
-            pltpu.SemaphoreType.DMA((10,)), pltpu.SemaphoreType.DMA((4,)), pltpu.SemaphoreType.DMA((4,)), pltpu.SemaphoreType.DMA((2,))],
+            pltpu.VMEM((8, 256, width), F32), pltpu.VMEM((6, GU_BLOCK * 40, 128), F32),
+            pltpu.SemaphoreType.DMA((10,)), pltpu.SemaphoreType.DMA((8,)), pltpu.SemaphoreType.DMA((6,)), pltpu.SemaphoreType.DMA((2,))],
         compiler_params=pltpu.CompilerParams(vmem_limit_bytes=56 << 20),
     )(*arrays, dg1, dg2)
 

time: 157 us -> 156 us (level)
  no operation moved by 1% of the time
where the time goes in v7:
time: 156 us
  Pallas kernels  155 us (99%)
    pallas_call x1, Pallas kernels, run_layer(): pl.pallas_call(layer_kernel, name='layer', out_shape=(act(width), act(wid...  132 us
    pallas_call x1, Pallas kernels, weight_grads(): pl.pallas_call(grads_kernel, name='weight_grads', in_specs=[any_spec] * 1...  23.3 us

profile of v7, /device:TPU:0, one launch (start us, length us, event | category | flops | bytes accessed | tf_op | source)
XLA Modules:
  0.0 155.6 jit_solution(8118556848738818139)
XLA Ops:
  0.6 131.5 %layer.1 = (bf16[256,1536]{1,0:T(8,128)(2,1)}, bf16[256,1536]{1,0:T(8,128)(2,1)}, f32[1,1536]{1,0:T(1,128)}, f32[1,1536]{1,0:T(1,128)}, bf16[256,1536]{1,0:T(8,1...) custom-call(bf16[256,1536]{1,0:T(8,128)(2,1)} %x_hbm.1, ...), custom_call_target="tpu_custom_call" | custom-call | tf_op jit(solution)/shard_map/layer/pallas_call | solution.py:689
  132.2 23.3 %weight_grads.1 = (f32[2048,1536]{1,0:T(8,128)}, f32[1536,32,128]{2,1,0:T(8,128)}, f32[768,1536]{1,0:T(8,128)}, f32[2304,1536]{1,0:T(8,128)}, bf16[256,1536]{1,0...) custom-call(bf16[256,2048]{1,0:T(8,128)(2,1)} %get-tuple-element.27.act_hbm, ...), custom_call_target="tpu_custom_call" | custom-call | tf_op jit(solution)/shard_map/weight_grads/pallas_call | solution.py:801

commit v8 on v7

--- a/solution.py
+++ b/solution.py
@@ -74,9 +74,10 @@
     def load(src, dst, sem):
         return pltpu.make_async_copy(src, dst, load_sem.at[sem])
 
-    loads = [load(x_hbm, x_ref, 0), load(dy_hbm, dy_ref, 1), load(wdown_hbm, wdown_ref, 2),
-             load(wqkv_hbm, wqkv_ref, 3), load(wout_hbm, wout_ref, 4)]
-    for copy in loads[:3]:
+    first, rest = pl.ds(0, ff // 8), pl.ds(ff // 8, ff - ff // 8)
+    loads = [load(x_hbm, x_ref, 0), load(dy_hbm, dy_ref, 1), load(wdown_hbm.at[first], wdown_ref.at[first], 2),
+             load(wqkv_hbm, wqkv_ref, 3), load(wout_hbm, wout_ref, 4), load(wdown_hbm.at[rest], wdown_ref.at[rest], 5)]
+    for copy in loads[:4]:
         copy.start()
 
     raw_rows = raw_ref.shape[1]
@@ -223,33 +224,31 @@
             total = total + dots_ref[k, n, 0:1, :]
         return jnp.broadcast_to(total, (128, rows)).T[:, 0:1]
 
+    def ga_body(k, carry):
+        cols = step(k, ga_cols)
+        ga_send[:, cols] = dot_nt(dy_ref[...], wdown_ref[cols, :]).astype(BF)
+        return carry
+
+    loads[0].wait()
+    x32 = x_ref[...].astype(F32)
+    sq1 = jnp.sum(x32 * x32, axis=-1, keepdims=True)
+    loads[1].wait()
+    loads[2].wait()
+    ga_body(0, 0)
+    pl.semaphore_wait(barrier, 7)
+    stat_put(0, sq1, tokens)
+    ga_copy(0).start()
+    for copy in loads[4:]:
+        copy.start()
+    for slot in range(2):
+        raw_load(slot, slot).start()
+    g1_ref[...] = g1_in[...].reshape(1, width)
+    g2_ref[...] = g2_in[...].reshape(1, width)
     place = pos_in[...].reshape(1, tokens).astype(F32)
     pair_i = lax.broadcasted_iota(jnp.int32, (HALF, 1), 0).astype(F32)
     angles = jnp.exp(pair_i * (-2.0 * math.log(ROPE_BASE) / HEAD)) * place
     cos_ref[...] = jnp.cos(angles)
     sin_ref[...] = jnp.sin(angles)
-    g1_ref[...] = g1_in[...].reshape(1, width)
-    g2_ref[...] = g2_in[...].reshape(1, width)
-    loads[0].wait()
-    x32 = x_ref[...].astype(F32)
-    sq1 = jnp.sum(x32 * x32, axis=-1, keepdims=True)
-    for copy in loads[3:]:
-        copy.start()
-    for slot in range(2):
-        raw_load(slot, slot).start()
-
-    def ga_body(k, carry):
-        cols = step(k, ga_cols)
-        ga_send[:, cols] = dot_nt(dy_ref[...], wdown_ref[cols, :]).astype(BF)
-        return carry
-
-    loads[1].wait()
-    loads[2].wait()
-    lax.fori_loop(0, 4, ga_body, 0)
-    pl.semaphore_wait(barrier, 7)
-    stat_put(0, sq1, tokens)
-    ga_copy(0).start()
-    lax.fori_loop(4, 8, ga_body, 0)
     inv1 = lax.rsqrt(stat_get(0, tokens) / full_width + EPSILON)
     inv1_ref[...] = inv1
     r1_ref[...] = (x_ref[...].astype(F32) * inv1 * g1_ref[...]).astype(BF)
@@ -272,6 +271,8 @@
 
     lax.fori_loop(0, half_heads, qkv_theirs, 0)
     lax.fori_loop(0, half_heads, qkv_mine, 0)
+    loads[5].wait()
+    lax.fori_loop(1, 8, ga_body, 0)
 
     row_i = lax.broadcasted_iota(jnp.int32, (256, 256), 0)
     col_i = lax.broadcasted_iota(jnp.int32, (256, 256), 1)
@@ -578,7 +579,6 @@
         dg1_ref[...] += jnp.sum(gin * unit, axis=0, keepdims=True)
 
     def rest_of_gate_up():
-        gu_start(EARLY, 2)
         gu_start(EARLY, 3)
 
     mlp_pieces(LATE, 0, GU_PIECES)
@@ -588,6 +588,7 @@
     down_chunk(LATE)
     stage3(AR_R2, LATE)
     stage2(AR_Y, LATE)
+    gu_start(EARLY, 2)
     hidden_back(LATE, rest_of_gate_up)
     mlp_pieces(EARLY, 0, 2)
     stage3(AR_Y, LATE)
@@ -605,10 +606,10 @@
     gm_copy(LATE, 1 - emb).wait_recv()
     lax.fori_loop(0, 2, late_theirs, 0)
     stage3(AR_R2, EARLY)
+    stage2(AR_Y, EARLY)
     hidden_back(EARLY)
     stores.append(store(dh_ref, dh_hbm, 5))
     stores.append(store(dg2_ref, dg2_hbm, 6))
-    stage2(AR_Y, EARLY)
     lax.fori_loop(2, half_heads, late_theirs, 0)
     input_cot(LATE)
     gm_copy(EARLY, 0).wait_recv()
@@ -679,7 +680,7 @@
         pltpu.VMEM((3, 8, tokens), F32), pltpu.VMEM((3, 8, tokens), F32),
         pltpu.VMEM((3, tokens, width), BF), pltpu.VMEM((3, tokens, width // 2), BF), pltpu.VMEM((3, tokens, width // 2), BF),
         pltpu.VMEM((3, tokens, width // 2), BF), pltpu.VMEM((3, tokens, width), BF),
-        pltpu.SemaphoreType.DMA((5,)), pltpu.SemaphoreType.DMA((2,)), pltpu.SemaphoreType.DMA((10 + CHUNKS,)),
+        pltpu.SemaphoreType.DMA((6,)), pltpu.SemaphoreType.DMA((2,)), pltpu.SemaphoreType.DMA((10 + CHUNKS,)),
     ]
     half_heads = heads // 2
     for n in (3, 3, 1, 1, 1, half_heads, CHUNKS, GU_PIECES * CHUNKS, CHUNKS, 2 * CHUNKS, 4, 4 * CHUNKS, 4 * CHUNKS, 4 * CHUNKS, 4, 4 * CHUNKS,

time: 156 us -> 152 us (0.974)
  Pallas kernels: 155 us -> 150 us
    pallas_call x1, Pallas kernels: 132 us -> 127 us  [run_layer(): pl.pallas_call(layer_kernel, name='layer', out_shape=(act(width), act(wid...]
where the time goes in v8:
time: 152 us; the launch traced here: 151 us
  Pallas kernels  150 us (99%)
    pallas_call x1, Pallas kernels, run_layer(): pl.pallas_call(layer_kernel, name='layer', out_shape=(act(width), act(wid...  127 us
    pallas_call x1, Pallas kernels, weight_grads(): pl.pallas_call(grads_kernel, name='weight_grads', in_specs=[any_spec] * 1...  23.3 us

profile of v8, /device:TPU:0, one launch (start us, length us, event | category | flops | bytes accessed | tf_op | source)
XLA Modules:
  0.0 151.2 jit_solution(1020049258800467036)
XLA Ops:
  0.6 127.1 %layer.1 = (bf16[256,1536]{1,0:T(8,128)(2,1)}, bf16[256,1536]{1,0:T(8,128)(2,1)}, f32[1,1536]{1,0:T(1,128)}, f32[1,1536]{1,0:T(1,128)}, bf16[256,1536]{1,0:T(8,1...) custom-call(bf16[256,1536]{1,0:T(8,128)(2,1)} %x_hbm.1, ...), custom_call_target="tpu_custom_call" | custom-call | tf_op jit(solution)/shard_map/layer/pallas_call | solution.py:690
  127.7 23.3 %weight_grads.1 = (f32[2048,1536]{1,0:T(8,128)}, f32[1536,32,128]{2,1,0:T(8,128)}, f32[768,1536]{1,0:T(8,128)}, f32[2304,1536]{1,0:T(8,128)}, bf16[256,1536]{1,0...) custom-call(bf16[256,2048]{1,0:T(8,128)(2,1)} %get-tuple-element.27.act_hbm, ...), custom_call_target="tpu_custom_call" | custom-call | tf_op jit(solution)/shard_map/weight_grads/pallas_call | solution.py:802

commit v9 on v8

--- a/solution.py
+++ b/solution.py
@@ -537,11 +537,11 @@
         late_heads((j,))
         return carry
 
-    def early_body(i, carry):
+    def early_heads(js):
         stored = []
         early = slice(0, rows)
         cos_t, sin_t = cos_ref[:, early], sin_ref[:, early]
-        for j in (2 * i, 2 * i + 1):
+        for j in js:
             r_q, r_k, r_v = head_rows(j)
             r_a = mix_rows(j)
             da = add_bf(gm_send[r_a, early], gm_recv[r_a, early])
@@ -553,7 +553,6 @@
                        (dqkv_ref, (r_k, early), unrope(dk.astype(BF), cos_t, sin_t)),
                        (dqkv_ref, (r_v, early), dv.astype(BF))]
         write(stored)
-        return carry
 
     def cot_product(c, lo, hi):
         return dot_tn(dqkv_ref[lo:hi, c * rows:(c + 1) * rows], wqkv_ref[lo:hi, :])
@@ -614,10 +613,10 @@
     input_cot(LATE)
     gm_copy(EARLY, 0).wait_recv()
     stage2(AR_R1, LATE)
-    lax.fori_loop(0, half_heads // 2, early_body, 0)
+    early_heads(range(half_heads))
     cot_ref[...] = cot_product(EARLY, 0, half_chans)
     gm_copy(EARLY, 1).wait_recv()
-    lax.fori_loop(half_heads // 2, half_heads, early_body, 0)
+    early_heads(range(half_heads, heads))
     input_cot(EARLY)
     stores.append(store(dqkv_ref, dqkv_hbm, 7))
     stage2(AR_R1, EARLY)

time: 152 us -> 152 us (level)
  no operation moved by 1% of the time
where the time goes in v9:
time: 152 us
  Pallas kernels  151 us (99%)
    pallas_call x1, Pallas kernels, run_layer(): pl.pallas_call(layer_kernel, name='layer', out_shape=(act(width), act(wid...  127 us
    pallas_call x1, Pallas kernels, weight_grads(): pl.pallas_call(grads_kernel, name='weight_grads', in_specs=[any_spec] * 1...  23.3 us

profile of v9, /device:TPU:0, one launch (start us, length us, event | category | flops | bytes accessed | tf_op | source)
XLA Modules:
  0.0 151.6 jit_solution(4110345310825677489)
XLA Ops:
  0.6 127.5 %layer.1 = (bf16[256,1536]{1,0:T(8,128)(2,1)}, bf16[256,1536]{1,0:T(8,128)(2,1)}, f32[1,1536]{1,0:T(1,128)}, f32[1,1536]{1,0:T(1,128)}, bf16[256,1536]{1,0:T(8,1...) custom-call(bf16[256,1536]{1,0:T(8,128)(2,1)} %x_hbm.1, ...), custom_call_target="tpu_custom_call" | custom-call | tf_op jit(solution)/shard_map/layer/pallas_call | solution.py:689
  128.1 23.3 %weight_grads.1 = (f32[2048,1536]{1,0:T(8,128)}, f32[1536,32,128]{2,1,0:T(8,128)}, f32[768,1536]{1,0:T(8,128)}, f32[2304,1536]{1,0:T(8,128)}, bf16[256,1536]{1,0...) custom-call(bf16[256,2048]{1,0:T(8,128)(2,1)} %get-tuple-element.27.act_hbm, ...), custom_call_target="tpu_custom_call" | custom-call | tf_op jit(solution)/shard_map/weight_grads/pallas_call | solution.py:801
